TPU v7x, 512 devices: a whole 4x4x16 slice. The times are simulated.
512 devices in a mesh: grp: 16 (over z), row: 32 (over x, y, core).
Axes of the slice: x: 4, y: 4, z: 16, core: 2. Of those that a mesh axis runs over, the one named last changes fastest.
Arguments:
- a_pieces: bfloat16 [16, 2048, 4096], P('grp', 'row'), as said below
- touched: int32 [16, 2048], P('grp', 'row'), may hold values from 0 to 7
- slot_row: int32 [2048], P('row'), may hold values from 0 to 2047, as said below
- x_blocks: bfloat16 [128, 64, 64], P('grp'), as said below
- z_inverse: bfloat16 [128, 64, 64], P('grp'), as said below
- block_class: int32 [128], P('grp'), may hold values from 0 to 1
Outputs:
- schur: float32 [2048, 2048], P('row', 'grp')
Inputs may be any that keep to these rules, and one draw needn't show every extreme that they name: `slot_row`: A permutation of the constraints. The 64 slots of one index r of row (slots r * 64 onward) hold, of the constraints o * 64 to (o + 1) * 64 - 1 of each index o, either none or exactly 4. `a_pieces`: each piece read as a 64 x 64 matrix is symmetric. `x_blocks`: each block is symmetric positive definite. `z_inverse`: each block is symmetric positive definite.
All inputs are finite; a program needn't handle non-finite values.
Results may differ from a plain program's by a relative error of at most 0.0008.
Values may be sent and summed in bfloat16 or wider, within the bound.
No kernel may reach another device: no remote copies, remote signals or barrier semaphores. Data moves between devices by JAX's collectives and lax.ppermute only.
A program may use at most 64 MiB of HBM per device.

v0:
```python
import jax
import jax.numpy as jnp
from jax import lax
from jax.sharding import PartitionSpec as P


def turned_gather(arrays, axis, dims):
    turned = [jnp.moveaxis(a, dim, 0) for a, dim in zip(arrays, dims)]
    widths = [t[0].size for t in turned]
    both = jnp.concatenate([t.reshape(-1, w) for t, w in zip(turned, widths)], axis=1)
    result = lax.all_gather(both, axis, axis=0, tiled=True)
    tiles = jnp.split(result, [sum(widths[:k]) for k in range(1, len(widths))], axis=1)
    return tuple(
        (
            jnp.moveaxis(b.reshape(-1, *t.shape[1:]), 0, dim)
            for b, t, dim in zip(tiles, turned, dims)
        )
    )


def in_blocks(value, dim, peers):
    shape = value.shape
    tiles = value.reshape(*shape[:dim], peers, shape[dim] // peers, *shape[dim + 1 :])
    return jnp.moveaxis(tiles, dim, 0)


def sent_and_summed(value, axis, dim):
    tiles = in_blocks(value, dim, lax.axis_size(axis))
    arrived = lax.all_to_all(tiles, axis, split_axis=0, concat_axis=0, tiled=True)
    return arrived.sum(axis=0)


def masked_blocks(blocks, block_class):
    block_order = blocks.shape[1]
    positions = jnp.arange(block_order)
    active = block_order // 2 * (1 + block_class)
    inside = (positions[None, :, None] < active[:, None, None]) & (
        positions[None, None, :] < active[:, None, None]
    )
    return jnp.where(inside, blocks, jnp.zeros_like(blocks))


def shards(a_pieces, touched, slot_row, x_blocks, z_inverse, block_class):
    local_rows = a_pieces.shape[1]
    block_order = x_blocks.shape[1]
    flat_len = a_pieces.shape[2]
    x_masked = masked_blocks(x_blocks, block_class)
    z_masked = masked_blocks(z_inverse, block_class)
    own_block = touched[0]
    a_local = a_pieces[0]
    pieces = a_local.reshape(local_rows, block_order, block_order)
    left_part = jnp.einsum(
        "rab,rbc->rac", x_masked[own_block], pieces, preferred_element_type=jnp.float32
    ).astype(jnp.bfloat16)
    product = jnp.einsum(
        "rab,rbc->rac", left_part, z_masked[own_block], preferred_element_type=jnp.float32
    ).astype(jnp.bfloat16)
    product_flat = product.reshape(local_rows, flat_len)
    all_slots, all_kinds = turned_gather((slot_row, touched), "row", (0, 1))
    constraints = all_slots.shape[0]
    kinds_flat = all_kinds[0]
    scores = lax.dot_general(
        product_flat,
        lax.all_gather(a_local, "row", axis=0, tiled=True),
        (((1,), (1,)), ((), ())),
        preferred_element_type=jnp.float32,
    )
    scores = jnp.where(own_block[:, None] == kinds_flat[None, :], scores, jnp.zeros_like(scores))
    inverse = (
        jnp.zeros((constraints,), jnp.int32)
        .at[all_slots]
        .set(jnp.arange(constraints, dtype=jnp.int32))
    )
    ordered = scores[:, inverse]
    summed = sent_and_summed(ordered, "grp", 1)
    columns = summed.shape[1]
    devices = lax.axis_size("row")
    slot_cap = max(2, local_rows // devices * 2)
    owners = slot_row // local_rows
    earlier = jnp.arange(local_rows)[None, :] < jnp.arange(local_rows)[:, None]
    rank_send = jnp.sum(((owners[:, None] == owners[None, :]) & earlier).astype(jnp.int32), axis=1)
    send_slot = owners * slot_cap + rank_send
    outgoing = jnp.zeros((devices * slot_cap, columns), jnp.float32).at[send_slot].set(summed)
    incoming = lax.all_to_all(outgoing, "row", split_axis=0, concat_axis=0, tiled=True)
    my_row = lax.axis_index("row")
    table_ids = all_slots.reshape(devices, local_rows)
    arrives = table_ids // local_rows == my_row
    rank_recv = jnp.cumsum(arrives.astype(jnp.int32), axis=1) - 1
    source_base = (jnp.arange(devices, dtype=jnp.int32) * slot_cap)[:, None]
    target = jnp.where(arrives, source_base + rank_recv, devices * slot_cap)
    landing = jnp.full((devices * slot_cap + 1,), local_rows, jnp.int32)
    landing = landing.at[target.reshape(-1)].set((table_ids % local_rows).reshape(-1))
    result = (
        jnp.zeros((local_rows, columns), jnp.float32).at[landing[:-1]].set(incoming, mode="drop")
    )
    return result


def solution(mesh):
    return jax.shard_map(
        shards,
        mesh=mesh,
        in_specs=(
            P("grp", "row", None),
            P("grp", "row"),
            P("row"),
            P("grp", None, None),
            P("grp", None, None),
            P("grp"),
        ),
        out_specs=P("row", "grp"),
        check_vma=False,
    )
```

profile of v0, /device:TPU:1, one launch (start us, length us, event | category | flops | bytes accessed | tf_op | source)
XLA Modules:
  0.0 185.9 jit_solution(13201511744794542731)
XLA Ops:
  6.5 0.7 all-gather.4.cloned.1.call-update
  7.3 2.1 %reshape_squeeze.3 = bf16[64,64,64]{2,1,0:T(8,128)(2,1)S(1)} reshape(bf16[1,64,4096]{2,1,0:T(8,128)(2,1)} %param.6) | data formatting | bytes 1048576 | tf_op jit(solution)/shard_map/reshape;squeeze | solution.py:51
  9.3 0.7 add_bitcast_fusion
  10.0 27.1 %all-gather.1 = s32[32,64,2]{1,2,0:T(2,128)S(1)} all-gather(s32[1,64,2]{1,2,0:T(2,128)S(1)} %add_bitcast_fusion), channel_id=1, replica_groups=mesh['grp'=16,'row'=32] {'row'}, dimensions={0}, use_global_device_ids=true | all-gather | bytes 16896 | tf_op jit(solution)/shard_map/all_gather | solution.py:11
  37.2 0.7 fusion.18
  37.9 0.7 add_multiply_fusion
  38.6 1.1 and_select_fusion.1
  39.7 0.7 gather_fusion.1
  40.5 0.7 gather_fusion
  41.3 1.7 convolution_convert_fusion
  43.0 2.1 %reshape.123 = bf16[64,4096]{1,0:T(8,128)(2,1)S(1)} reshape(bf16[64,64,64]{2,1,0:T(8,128)(2,1)} %convolution_convert_fusion) | data formatting | bytes 1048576 | tf_op jit(solution)/shard_map/reshape | solution.py:58
  45.1 8.0 %scatter_custom_fusion.1 = s32[2048]{0:T(1024)S(1)} fusion(s32[2048]{0:T(1024)S(1)} %bitcast.34, s32[2048]{0:T(1024)S(1)} %iota.33, s32[]{:T(128)} %constant.35.clone.1), kind=kCustom, calls=%fused_computation.46 | custom fusion | bytes 8196 | tf_op jit(solution)/shard_map/scatter | solution.py:72
  53.2 50.9 %all-gather.4.cloned.1.call-done = bf16[1,2048,4096]{2,1,0:T(8,128)(2,1)} async-done(((bf16[1,64,4096]{2,1,0:T(8,128)(2,1)}), bf16[1,2048,4096]{2,1,0:T(8,128)(2,1)}) %all-gather.4.cloned.1.call-update) | async-done | bytes 16777232 | tf_op jit(solution)/shard_map/all_gather | solution.py:64
  104.0 11.0 %fusion.2 = f32[64,2048]{1,0:T(8,128)S(1)} fusion(bf16[64,4096]{1,0:T(8,128)(2,1)S(1)} %reshape.123, bf16[1,2048,4096]{2,1,0:T(8,128)(2,1)} %all-gather.4.cloned.1.call-done, s32[2048]{0:T(1024)S(1)} %bitcast.31, s32[64]{0:T(128)} %bitcast.36), kind=kOutput, calls=%fused_computation.9 | convolution fusion | flops 1074003968 | bytes 17834240 | tf_op jit(solution)/shard_map/dot_general | solution.py:62
  115.0 0.3 copy.20
  115.3 5.5 %gather_fusion.2 = f32[2048,64]{1,0:T(8,128)S(1)} fusion(f32[64,2048]{0,1:T(8,128)S(1)} %copy.20, s32[2048]{0:T(1024)S(1)} %fusion.15), kind=kCustom, calls=%fused_computation.2 | custom fusion | bytes 1056768 | tf_op jit(solution)/shard_map/gather | solution.py:74
  120.8 1.1 copy.21
  121.9 12.0 %all-to-all-start = ((f32[16,64,128]{2,1,0:T(8,128)}), f32[16,64,128]{2,1,0:T(8,128)S(1)}, u32[]{:S(2)}, u32[]{:S(2)}) async-start(f32[16,64,128]{2,1,0:T(8,128)} %bitcast.12), calls=%async_computation | async-start | bytes 1048576 | tf_op jit(solution)/shard_map/all_to_all | solution.py:29
  134.5 8.0 %scatter_custom_fusion = s32[129]{0:T(256)S(1)} fusion(s32[2048]{0:T(1024)S(1)} %bitcast.33, s32[2048]{0:T(1024)S(1)} %add_select_fusion.1, s32[]{:T(128)} %constant.32.clone.1), kind=kCustom, calls=%fused_computation.59 | custom fusion | bytes 520 | tf_op jit(solution)/shard_map/scatter | solution.py:92
  142.8 13.8 %all-to-all-done = f32[16,64,128]{2,1,0:T(8,128)S(1)} async-done(((f32[16,64,128]{2,1,0:T(8,128)}), f32[16,64,128]{2,1,0:T(8,128)S(1)}, u32[]{:S(2)}, u32[]{:S(2)}) %all-to-all-start) | async-done | bytes 524320 | tf_op jit(solution)/shard_map/all_to_all | solution.py:29
  156.6 1.3 scatter_custom_fusion.2
  157.9 12.3 %all-to-all-start.1 = ((f32[32,4,128]{2,1,0:T(4,128)}), f32[32,4,128]{2,1,0:T(4,128)S(1)}, u32[]{:S(2)}, u32[]{:S(2)}) async-start(f32[32,4,128]{2,1,0:T(4,128)} %bitcast.13), calls=%async_computation.1 | async-start | bytes 131072 | tf_op jit(solution)/shard_map/all_to_all | solution.py:84
  170.2 7.4 %all-to-all-done.1 = f32[32,4,128]{2,1,0:T(4,128)S(1)} async-done(((f32[32,4,128]{2,1,0:T(4,128)}), f32[32,4,128]{2,1,0:T(4,128)S(1)}, u32[]{:S(2)}, u32[]{:S(2)}) %all-to-all-start.1) | async-done | bytes 65568 | tf_op jit(solution)/shard_map/all_to_all | solution.py:84
  177.6 1.4 scatter_custom_fusion.3
  (23 shorter events, 1.0 us)
Async XLA Ops:
  6.5 97.5 %all-gather.4.cloned.1.call-start = ((), (), s32[]{:S(2)}) async-start(), calls=%async_computation.2 | async-start | bytes 17301504 | tf_op jit(solution)/shard_map/all_gather | solution.py:64
  41.2 101.3 %copy-start = (s32[64]{0:T(128)S(1)}, s32[64]{0:T(128)}, u32[]{:S(2)}) copy-start(s32[64]{0:T(128)} %param.8) | copy-start | bytes 772
  121.9 34.7 %all-to-all-start = ((f32[16,64,128]{2,1,0:T(8,128)}), f32[16,64,128]{2,1,0:T(8,128)S(1)}, u32[]{:S(2)}, u32[]{:S(2)}) async-start(f32[16,64,128]{2,1,0:T(8,128)} %bitcast.12), calls=%async_computation | async-start | bytes 1048576 | tf_op jit(solution)/shard_map/all_to_all | solution.py:29
  157.9 19.6 %all-to-all-start.1 = ((f32[32,4,128]{2,1,0:T(4,128)}), f32[32,4,128]{2,1,0:T(4,128)S(1)}, u32[]{:S(2)}, u32[]{:S(2)}) async-start(f32[32,4,128]{2,1,0:T(4,128)} %bitcast.13), calls=%async_computation.1 | async-start | bytes 131072 | tf_op jit(solution)/shard_map/all_to_all | solution.py:84
Sparse Core Ops, SparseCore 0:
  10.5 93.5 all-gather.3
where the time goes:
time: 186 us
  waiting for transfers between devices  72.8 us (39%)
  local copies, waits for them, and re-layouts  31.6 us (17%)
  blocking collectives  27.1 us (15%)
  starting transfers between devices  24.3 us (13%)
  between operations  13.6 us (7%)
  matrix products  12.7 us (7%)
  other arithmetic  3.86 us (2%)
    all_gather x1, waiting for transfers between devices, shards(): lax.all_gather(a_local, 'row', axis=0, tiled=True)  50.9 us
    all_gather x1, blocking collectives, turned_gather(): result = lax.all_gather(both, axis, axis=0, tiled=True)  27.1 us
    all_to_all x1, waiting for transfers between devices, sent_and_summed(): lax.all_to_all(tiles, axis, split_axis=0, concat_axis=0, tiled=True)  13.8 us
    all_to_all x1, starting transfers between devices, shards(): lax.all_to_all(outgoing, 'row', split_axis=0, concat_axis=0, tiled=True)  12.3 us
    all_to_all x1, starting transfers between devices, sent_and_summed(): lax.all_to_all(tiles, axis, split_axis=0, concat_axis=0, tiled=True)  12 us
    dot_general x1, matrix products, shards(): lax.dot_general(product_flat, lax.all_gather(a_local, 'row', axis=0, tile...  11 us
    scatter x1, local copies, waits for them, and re-layouts, shards(): inverse = jnp.zeros((constraints,), jnp.int32).at[all_slots].set(jnp.aran...  8.05 us
    scatter x1, local copies, waits for them, and re-layouts, shards(): landing.at[target.reshape(-1)].set((table_ids % local_rows).reshape(-1))  8.04 us
  transfers between devices with their start and end apart: 3, of which 3 were waited for; matrix products, arithmetic and copies ran while one was open for 15% of the time, Pallas kernels for 0%

commit v1 on v0

v1 whole, which is shorter than its diff:
```python
import functools
import jax
import jax.numpy as jnp
from jax import lax
from jax.experimental import pallas as pl
from jax.experimental.pallas import tpu as pltpu
from jax.sharding import PartitionSpec as P

F32 = jnp.float32
BF16 = jnp.bfloat16
HI = lax.Precision.HIGHEST
NB = 64
CHUNKS = 17
WIDTH = CHUNKS * 128
ROWS = 64
SIDE = 4
DEPTH = 80
Z_TYPE = jnp.float32
VMEM = pl.BlockSpec(memory_space=pltpu.VMEM)
SMEM = pl.BlockSpec(memory_space=pltpu.SMEM)


def iota(shape, dim):
    return lax.broadcasted_iota(jnp.int32, shape, dim)


def ones_where(cond, dtype=F32):
    return jnp.where(cond, 1.0, 0.0).astype(dtype)


def nt(a, b, precision=None):
    return lax.dot_general(a, b, (((1,), (1,)), ((), ())), precision=precision, preferred_element_type=F32)


def tn(a, b, precision=None):
    return lax.dot_general(a, b, (((0,), (0,)), ((), ())), precision=precision, preferred_element_type=F32)


def nn(a, b, precision=None):
    return lax.dot_general(a, b, (((1,), (0,)), ((), ())), precision=precision, preferred_element_type=F32)


def folded(read, weigh):
    lane = iota((ROWS, 128), 1)
    column = lane & (NB - 1)
    chunks = []
    spill = jnp.zeros((ROWS, 128), F32)
    for q in range(16):
        low = read(q)
        high = read(31 - q)
        if weigh:
            low = jnp.where((column >> 1) == q, low * 0.5, low)
        turned = pltpu.roll(high, 2 * q, 1) if q else high
        chunks.append(jnp.where(column >= 2 * q, low, turned))
        block = (column >> 1) == (31 - q)
        spill = jnp.where(block, high * 0.5 if weigh else high, spill)
    return chunks, spill


def pack_kernel(a_ref, p_ref, slot_ref, touched_ref, out_ref):
    r = iota((ROWS, ROWS), 0)
    c = iota((ROWS, ROWS), 1)

    def as_column(row):
        return jnp.sum(jnp.where(r == c, row, 0.0), axis=1, keepdims=True)

    slot = slot_ref[...]
    owner_row = (slot >> 6).astype(F32)
    inner_row = (slot & (ROWS - 1)).astype(F32)
    touched_row = touched_ref[...].astype(F32)
    owner_full = jnp.broadcast_to(owner_row, (ROWS, ROWS))
    owner_col = as_column(owner_full)
    inner_col = as_column(jnp.broadcast_to(inner_row, (ROWS, ROWS)))
    touched_col = as_column(jnp.broadcast_to(touched_row, (ROWS, ROWS)))
    rank = jnp.sum(ones_where((owner_col == owner_full) & (r < c)), axis=0, keepdims=True)
    lower = jnp.sum(ones_where(owner_col < owner_full), axis=0, keepdims=True)
    place = rank * 16.0 + lower * 0.25
    select = ones_where(r.astype(F32) == place, BF16)
    lane = iota((ROWS, 128), 1)

    def with_ids(spill, first):
        ids = jnp.where(lane == first, touched_col, jnp.where(lane == first + 1, owner_col, inner_col))
        return jnp.where((lane & (NB - 1)) >= 32, spill, jnp.where((lane >= first) & (lane < first + 3), ids, 0.0))

    chunks, spill = folded(lambda q: a_ref[:, q * 128 : (q + 1) * 128].astype(F32), False)
    chunks.append(with_ids(spill, 0))
    for q, chunk in enumerate(chunks):
        picked = nn(select, chunk.astype(BF16)).astype(BF16)
        for k in range(SIDE):
            out_ref[k, 0:16, q * 128 : (q + 1) * 128] = picked[16 * k : 16 * (k + 1)]
    chunks, spill = folded(lambda q: p_ref[:, q * 128 : (q + 1) * 128].astype(F32), True)
    chunks.append(with_ids(spill, 3))
    for q, chunk in enumerate(chunks):
        rounded = chunk.astype(BF16)
        for k in range(SIDE):
            out_ref[k, 16:80, q * 128 : (q + 1) * 128] = rounded


def score_kernel(core_ref, rows_ref, near_ref, far_ref, out_ref, col_ref, row_ref):
    n_rows, n_cols = 256, 512
    rows = jnp.concatenate([rows_ref[k, 16:80, :] for k in range(SIDE)], axis=0)
    near = near_ref[...].reshape(256, WIDTH)
    far = far_ref[...].reshape(256, WIDTH)
    scores = jnp.concatenate([nt(near, rows), nt(far, rows)], axis=0)
    last = slice(16 * 128, WIDTH)
    col_ids = jnp.concatenate([near[:, last], far[:, last]], axis=0)
    row_ids = rows[:, last]
    pick = iota((8, 128), 0)
    spot = iota((8, 128), 1)
    col_t = nt(ones_where(pick == spot, BF16), col_ids)
    row_t = nt(ones_where(pick + 3 == spot, BF16), row_ids)
    lane_c = iota((n_cols, 128), 1).astype(F32)
    lane_r = iota((n_rows, 128), 1).astype(F32)
    col_f = col_ids.astype(F32)
    row_f = row_ids.astype(F32)
    kind_c = ones_where(col_f[:, 0:1] == lane_c, BF16)
    kind_r = ones_where(row_f[:, 3:4] == lane_r, BF16)
    same_kind = nt(kind_c, kind_r)
    scores = jnp.where(same_kind > 0.5, scores, 0.0)
    own_c = ones_where(col_f[:, 1:2] == lane_c, BF16)
    i = iota((n_cols, n_cols), 0)
    j = iota((n_cols, n_cols), 1)
    same = nt(own_c, own_c)
    turn = core_ref[0] * 256
    rank_c = jnp.sum(jnp.where((i ^ turn) < (j ^ turn), same, 0.0), axis=0, keepdims=True)
    place = col_t[1:2, :] * 16.0 + rank_c
    move = ones_where(i.astype(F32) == place)
    out_ref[...] = nn(move, scores, HI).astype(out_ref.dtype)
    odd = col_t[1:2, :] - 2.0 * jnp.floor(col_t[1:2, :] * 0.5)
    col_id = odd * 64.0 + col_t[2:3, :]
    col_ref[...] = nt(jnp.broadcast_to(col_id, (8, n_cols)), move, HI)
    own_r = ones_where(row_f[:, 4:5] == lane_r, BF16)
    ri = iota((n_rows, n_rows), 0)
    rj = iota((n_rows, n_rows), 1)
    same_r = nt(own_r, own_r)
    rank_r = jnp.sum(jnp.where((ri < rj) & ((ri >> 6) == (rj >> 6)), same_r, 0.0), axis=0, keepdims=True)
    line = (iota((1, n_rows), 1) >> 6).astype(F32)
    row_ref[0:1, :] = row_t[1:2, :] * 8.0 + line
    row_ref[1:2, :] = rank_r
    row_ref[2:3, :] = row_t[2:3, :] + 1.0
    row_ref[3:8, :] = jnp.zeros((5, n_rows), F32)


def send_kernel(group_ref, z_ref, col_ref, row_ref, out_ref):
    total = z_ref[0].astype(F32)
    for g in range(1, z_ref.shape[0]):
        total = total + z_ref[g].astype(F32)
    m = iota((256, 256), 0).astype(F32)
    target = row_ref[0:1, :]
    rank = row_ref[1:2, :]
    inner = jnp.broadcast_to(row_ref[2:3, :], (8, 256))
    s = iota((512, 128), 0)
    lane = iota((512, 128), 1)
    here = ones_where(s == group_ref[0] * 32 + (lane & 31))
    cols = nn(col_ref[...], here, HI)[0:1, :]
    values, indices = [], []
    for k in range(SIDE):
        values.append(nt(ones_where((m == target) & (rank == float(k))), total, HI))
        found = nt(ones_where((m == target + 4.0) & (rank == float(k))), inner, HI)
        indices.append(jnp.broadcast_to(found[:, 0:1], (256, 32)))
    value = jnp.concatenate(values, axis=1)
    index = jnp.concatenate(indices, axis=1) * 128.0 + cols
    is_id = (iota((256, 128), 0) & 7) >= 4
    out_ref[...] = jnp.where(is_id, index, value)


def land_kernel(in_ref, out_ref):
    parts = [in_ref[64 * x : 64 * (x + 1), :] for x in range(SIDE)]
    lane = iota((64, 512), 1)
    wide = jnp.concatenate(parts, axis=1)
    index = parts[0]
    high = jnp.floor(index * (1.0 / 128.0))
    high = pltpu.roll(high, 60, 0)
    is_value = (iota((64, 64), 0) & 7) < 4
    spot = iota((64, 64), 1).astype(F32) + 1.0
    total = None
    for k in range(SIDE):
        place = ones_where(is_value & (high[:, 32 * k : 32 * k + 1] == spot))
        part = tn(place, jnp.where(((lane >> 5) & 3) == k, wide, 0.0), HI)
        total = part if total is None else total + part
    id_row = wide[4:5, :]
    col = id_row - 128.0 * jnp.floor(id_row * (1.0 / 128.0))
    spread = ones_where(iota((128, 512), 0).astype(F32) == col)
    out_ref[...] = nt(total, spread, HI)


def call(kernel, out, n, first=VMEM):
    many = isinstance(out, tuple)
    return pl.pallas_call(
        kernel,
        out_shape=out,
        in_specs=[first] + [VMEM] * (n - 1),
        out_specs=tuple(VMEM for _ in out) if many else VMEM,
    )


def masked_blocks(blocks, block_class):
    block_order = blocks.shape[1]
    positions = jnp.arange(block_order)
    active = block_order // 2 * (1 + block_class)
    inside = (positions[None, :, None] < active[:, None, None]) & (
        positions[None, None, :] < active[:, None, None]
    )
    return jnp.where(inside, blocks, jnp.zeros_like(blocks))


def device(x, y, c):
    return (x * SIDE + y) * 2 + c


LINES_X = [[device(x, y, c) for x in range(SIDE)] for y in range(SIDE) for c in range(2)]
LINES_Y = [[device(x, y, c) for y in range(SIDE)] for x in range(SIDE) for c in range(2)]
SWAP = [(device(x, y, c), device(x, y, 1 - c)) for x in range(SIDE) for y in range(SIDE) for c in range(2)]


def shards(a_pieces, touched, slot_row, x_blocks, z_inverse, block_class):
    x_masked = masked_blocks(x_blocks, block_class)
    z_masked = masked_blocks(z_inverse, block_class)
    own_block = touched[0]
    a_local = a_pieces[0]
    pieces = a_local.reshape(ROWS, NB, NB)
    left = jnp.einsum("rab,rbc->rac", x_masked[own_block], pieces, preferred_element_type=F32).astype(BF16)
    product = jnp.einsum("rab,rbc->rac", left, z_masked[own_block], preferred_element_type=F32)
    both = (product + jnp.swapaxes(product, 1, 2)).astype(BF16).reshape(ROWS, NB * NB)
    packed = call(pack_kernel, jax.ShapeDtypeStruct((SIDE, DEPTH, WIDTH), BF16), 4)(
        a_local, both, slot_row[None, :], touched
    )
    lined = lax.all_to_all(packed, "row", 0, 0, tiled=True, axis_index_groups=LINES_X)
    mine = lined[:, :16, :].reshape(ROWS, WIDTH)
    near = lax.all_to_all(
        jnp.broadcast_to(mine[None], (SIDE, ROWS, WIDTH)), "row", 0, 0, tiled=True, axis_index_groups=LINES_Y
    )
    far = lax.ppermute(near, "row", SWAP)
    core = (lax.axis_index("row").astype(jnp.int32) & 1).reshape(1)
    scores, cols, rows = call(
        score_kernel,
        (
            jax.ShapeDtypeStruct((512, 256), Z_TYPE),
            jax.ShapeDtypeStruct((8, 512), F32),
            jax.ShapeDtypeStruct((8, 256), F32),
        ),
        4,
        SMEM,
    )(core, lined, near, far)
    summed = lax.all_to_all(scores.reshape(16, 32, 256), "grp", 0, 0, tiled=True)
    group = lax.axis_index("grp").astype(jnp.int32).reshape(1)
    outgoing = call(send_kernel, jax.ShapeDtypeStruct((256, 128), F32), 4, SMEM)(group, summed, cols, rows)
    incoming = lax.all_to_all(outgoing.reshape(32, 8, 128), "row", 0, 0, tiled=True)
    return call(land_kernel, jax.ShapeDtypeStruct((64, 128), F32), 1)(incoming.reshape(256, 128))


def solution(mesh):
    return jax.shard_map(
        shards,
        mesh=mesh,
        in_specs=(
            P("grp", "row", None),
            P("grp", "row"),
            P("row"),
            P("grp", None, None),
            P("grp", None, None),
            P("grp"),
        ),
        out_specs=P("row", "grp"),
        check_vma=False,
    )
```

time: 186 us -> 136 us (0.73)
  waiting for transfers between devices: 72.8 us -> 25.2 us
  blocking collectives: 27.1 us -> 59.6 us
  local copies, waits for them, and re-layouts: 31.6 us -> 8.94 us
  Pallas kernels: 0 us -> 14.8 us
  between operations: 13.6 us -> 0.08 us
  matrix products: 12.7 us -> 2.25 us
  starting transfers between devices: 24.3 us -> 19.8 us
    all_to_all x0 -> x3, blocking collectives: none -> 59.6 us  [the longest x1 22.5 us: shards(): lax.all_to_all(jnp.broadcast_to(mine[None], (SIDE, ROWS, WIDTH)), 'row',...]
    all_gather x1 -> x0, waiting for transfers between devices: 50.9 us -> none  [shards(): lax.all_gather(a_local, 'row', axis=0, tiled=True)]
    all_gather x1 -> x0, blocking collectives: 27.1 us -> none  [turned_gather(): result = lax.all_gather(both, axis, axis=0, tiled=True)]
    scatter x4 -> x0, local copies, waits for them, and re-layouts: 18.8 us -> none  [the longest x1 8.05 us: shards(): inverse = jnp.zeros((constraints,), jnp.int32).at[all_slots].set(jnp.aran...]
    pallas_call x0 -> x4, Pallas kernels: none -> 14.8 us  [the longest x1 5.69 us: shards(): call(score_kernel, (jax.ShapeDtypeStruct((512, 256), Z_TYPE), jax.ShapeDt...]
    dot_general x2 -> x1, matrix products: 12.7 us -> 2.25 us  [shards(): jnp.einsum('rab,rbc->rac', left, z_masked[own_block], preferred_element_t...]
    all_to_all x2 -> x1, starting transfers between devices: 24.3 us -> 14.9 us  [shards(): lax.all_to_all(scores.reshape(16, 32, 256), 'grp', 0, 0, tiled=True)]
    gather x1 -> x0, local copies, waits for them, and re-layouts: 5.47 us -> none  [shards(): ordered = scores[:, inverse]]
  transfers between devices with their start and end apart: 3 -> 2, of which waited for: 3 -> 2; matrix products, arithmetic and copies ran while one was open for 15% -> 0% of each run, Pallas kernels for 0% -> 0%
where the time goes in v1:
time: 136 us; the launch traced here: 135 us
  blocking collectives  59.6 us (44%)
  waiting for transfers between devices  25.2 us (19%)
  starting transfers between devices  19.8 us (15%)
  Pallas kernels  14.8 us (11%)
  local copies, waits for them, and re-layouts  8.94 us (7%)
  other arithmetic  4.53 us (3%)
  matrix products  2.25 us (2%)
    all_to_all x1, waiting for transfers between devices, shards(): lax.all_to_all(scores.reshape(16, 32, 256), 'grp', 0, 0, tiled=True)  22.7 us
    all_to_all x1, blocking collectives, shards(): lax.all_to_all(jnp.broadcast_to(mine[None], (SIDE, ROWS, WIDTH)), 'row',...  22.5 us
    all_to_all x1, blocking collectives, shards(): lax.all_to_all(outgoing.reshape(32, 8, 128), 'row', 0, 0, tiled=True)  19.1 us
    all_to_all x1, blocking collectives, shards(): lax.all_to_all(packed, 'row', 0, 0, tiled=True, axis_index_groups=LINES_X)  18 us
    all_to_all x1, starting transfers between devices, shards(): lax.all_to_all(scores.reshape(16, 32, 256), 'grp', 0, 0, tiled=True)  14.9 us
    pallas_call x1, Pallas kernels, shards(): call(score_kernel, (jax.ShapeDtypeStruct((512, 256), Z_TYPE), jax.ShapeDt...  5.69 us
    ppermute x1, starting transfers between devices, shards(): far = lax.ppermute(near, 'row', SWAP)  4.85 us
    pallas_call x1, Pallas kernels, shards(): call(send_kernel, jax.ShapeDtypeStruct((256, 128), F32), 4, SMEM)  3.78 us
  transfers between devices with their start and end apart: 2, of which 2 were waited for; matrix products, arithmetic and copies ran while one was open for 0% of the time, Pallas kernels for 0%

profile of v1, /device:TPU:1, one launch (start us, length us, event | category | flops | bytes accessed | tf_op | source)
XLA Modules:
  0.0 135.2 jit_solution(4198148219997958739)
XLA Ops:
  0.0 0.7 add_multiply_fusion
  0.7 0.1 iota_compare_fusion
  0.7 0.7 fusion.2
  1.4 1.1 and_select_fusion.1
  2.5 0.7 gather_fusion
  3.3 1.6 %gather_fusion.1 = bf16[64,64,64]{2,1,0:T(8,128)(2,1)} fusion(bf16[8,64,64]{2,1,0:T(8,128)(2,1)S(1)} %get-tuple-element.12, s32[1024]{0:T(1024)S(1)} %pad_clamp_fusion), kind=kCustom, calls=%fused_computation.1 | custom fusion | bytes 1048832 | tf_op jit(solution)/shard_map/gather | solution.py:223
  4.9 2.1 %reshape_squeeze.3 = bf16[64,64,64]{2,1,0:T(8,128)(2,1)} reshape(bf16[1,64,4096]{2,1,0:T(8,128)(2,1)S(1)} %copy-done.2) | data formatting | bytes 1048576 | tf_op jit(solution)/shard_map/reshape;squeeze | solution.py:221
  7.1 2.2 %fusion.1 = f32[64,64,64]{2,1,0:T(8,128)S(1)} fusion(bf16[64,64,64]{2,1,0:T(8,128)(2,1)} %gather_fusion.1, bf16[64,64,64]{2,1,0:T(8,128)(2,1)S(1)} %gather_fusion, bf16[64,64,64]{2,1,0:T(8,128)(2,1)} %reshape_squeeze.3), kind=kOutput, calls=%fused_computation.5 | convolution fusion | flops 67371008 | bytes 2621440 | tf_op jit(solution)/shard_map/rab,rbc->rac/dot_general | solution.py:223
  9.3 1.9 %copy.7 = f32[64,64,64]{1,2,0:T(8,128)} copy(f32[64,64,64]{2,1,0:T(8,128)S(1)} %fusion.1) | data formatting | bytes 2097152 | tf_op jit(solution)/shard_map/rab,rbc->rac/dot_general | solution.py:223
  11.2 2.0 %fusion = bf16[64,64,64]{2,1,0:T(8,128)(2,1)S(1)} fusion(f32[64,64,64]{2,1,0:T(8,128)S(1)} %fusion.1, f32[64,64,64]{1,2,0:T(8,128)} %copy.7), kind=kLoop, calls=%fused_computation.3 | loop fusion | flops 524288 | bytes 2621440 | tf_op jit(solution)/shard_map/convert_element_type | solution.py:224
  13.2 1.6 %reshape.94.p_ref = bf16[64,4096]{1,0:T(8,128)(2,1)} reshape(bf16[64,64,64]{2,1,0:T(8,128)(2,1)S(1)} %fusion) | data formatting | bytes 1048576 | tf_op jit(solution)/shard_map/reshape | solution.py:224
  14.8 2.8 %shard_map.64 = bf16[4,80,2176]{2,1,0:T(8,128)(2,1)} custom-call(bf16[64,4096]{1,0:T(8,128)(2,1)} %bitcast.19, bf16[64,4096]{1,0:T(8,128)(2,1)} %reshape.94.p_ref, s32[1,64]{1,0:T(1,128)} %bitcast.24, s32[1,64]{1,0:T(1,128)} %touched_ref.1), custom_call_target="tpu_custom_call" | custom-call | tf_op jit(solution)/shard_map/pallas_call | solution.py:225
  17.6 18.0 %all_to_all.20.rows_ref = bf16[4,80,2176]{2,1,0:T(8,128)(2,1)S(1)} all-to-all(bf16[4,80,2176]{2,1,0:T(8,128)(2,1)} %shard_map.64), channel_id=1, replica_groups={{0,8,16,24},{1,9,17,25},{2,10,18,26},{3,11,19,27},{4,12,20,28},{5,13,21..., dimensions={0} | all-to-all | bytes 2785280 | tf_op jit(solution)/shard_map/all_to_all | solution.py:228
  35.7 0.1 broadcast_in_dim.8
  35.8 22.5 %all_to_all.21.near_ref = bf16[4,64,2176]{2,1,0:T(8,128)(2,1)S(1)} all-to-all(bf16[4,64,2176]{2,1,0:T(8,128)(2,1)S(1)} %broadcast_in_dim.8), channel_id=1, replica_groups={{0,2,4,6},{1,3,5,7},{8,10,12,14},{9,11,13,15},{16,18,20,22},{17,19,21,2..., dimensions={0} | all-to-all | bytes 2228224 | tf_op jit(solution)/shard_map/all_to_all | solution.py:230
  58.3 4.8 %collective-permute-start = (bf16[4,64,2176]{2,1,0:T(8,128)(2,1)S(1)}, bf16[4,64,2176]{2,1,0:T(8,128)(2,1)}, u32[]{:S(2)}, u32[]{:S(2)}) collective-permute-start(bf16[4,64,2176]{2,1,0:T(8,128)(2,1)S(1)} %all_to_all.21.near_ref), channel_id=1, source_target_pairs={{0,1},{1,0},{2,3},{3,2},{4,5},{5,4},{6,7},{7,6},{8,9},{9,8},{10,11... | collective-permute-start | bytes 3342344 | tf_op jit(solution)/shard_map/ppermute | solution.py:233
  63.1 2.5 %collective-permute-done.far_ref = bf16[4,64,2176]{2,1,0:T(8,128)(2,1)} collective-permute-done((bf16[4,64,2176]{2,1,0:T(8,128)(2,1)S(1)}, bf16[4,64,2176]{2,1,0:T(8,128)(2,1)}, u32[]{:S(2)}, u32[]{:S(2)}) %collective-permute-start) | collective-permute-done | bytes 1114144 | tf_op jit(solution)/shard_map/ppermute | solution.py:233
  65.6 5.7 %shard_map.65 = (f32[512,256]{1,0:T(8,128)}, f32[8,512]{1,0:T(8,128)}, f32[8,256]{1,0:T(8,128)}) custom-call(s32[1]{0:T(128)} %bitcast.1.core_ref, bf16[4,80,2176]{2,1,0:T(8,128)(2,1)} %copy-done, bf16[4,64,2176]{2,1,0:T(8,128)(2,1)} %copy-done.1, bf16[4,64,2176]{2,1,0:T(8,128)(2,1)} %collective-permute-done.far_ref), custom_call_target="tpu_custom_call" | custom-call | tf_op jit(solution)/shard_map/pallas_call | solution.py:235
  71.3 14.9 %all-to-all-start.2 = ((f32[16,32,256]{2,1,0:T(8,128)}), f32[16,32,256]{2,1,0:T(8,128)S(1)}, u32[]{:S(2)}, u32[]{:S(2)}) async-start(f32[16,32,256]{2,1,0:T(8,128)} %bitcast.22), calls=%async_computation.2 | async-start | bytes 1048576 | tf_op jit(solution)/shard_map/all_to_all | solution.py:245
  86.2 22.7 %all-to-all-done.2.z_ref = f32[16,32,256]{2,1,0:T(8,128)S(1)} async-done(((f32[16,32,256]{2,1,0:T(8,128)}), f32[16,32,256]{2,1,0:T(8,128)S(1)}, u32[]{:S(2)}, u32[]{:S(2)}) %all-to-all-start.2) | async-done | bytes 524320 | tf_op jit(solution)/shard_map/all_to_all | solution.py:245
  109.0 0.8 copy-done.3
  109.8 3.8 %shard_map.66 = f32[256,128]{1,0:T(8,128)} custom-call(s32[1]{0:T(128)} %bitcast.group_ref, f32[16,32,256]{2,1,0:T(8,128)} %copy-done.3, f32[8,512]{1,0:T(8,128)} %get-tuple-element.9.col_ref, f32[8,256]{1,0:T(8,128)} %get-tuple-element.10.row_ref), custom_call_target="tpu_custom_call" | custom-call | tf_op jit(solution)/shard_map/pallas_call | solution.py:247
  113.6 19.1 %all_to_all.22 = f32[32,8,128]{2,1,0:T(8,128)} all-to-all(f32[32,8,128]{2,1,0:T(8,128)} %bitcast.23), channel_id=1, replica_groups=mesh['grp'=16,'row'=32] {'row'}, dimensions={0} | all-to-all | bytes 262144 | tf_op jit(solution)/shard_map/all_to_all | solution.py:248
  132.7 2.5 %shard_map.67 = f32[64,128]{1,0:T(8,128)} custom-call(f32[256,128]{1,0:T(8,128)} %bitcast.21), custom_call_target="tpu_custom_call" | custom-call | tf_op jit(solution)/shard_map/pallas_call | solution.py:249
  (9 shorter events, 0.0 us)
Async XLA Ops:
  2.5 2.4 %copy-start.2 = (bf16[1,64,4096]{2,1,0:T(8,128)(2,1)S(1)}, bf16[1,64,4096]{2,1,0:T(8,128)(2,1)}, u32[]{:S(2)}) copy-start(bf16[1,64,4096]{2,1,0:T(8,128)(2,1)} %param.6) | copy-start | bytes 1572868
  35.6 30.0 %copy-start = (bf16[4,80,2176]{2,1,0:T(8,128)(2,1)}, bf16[4,80,2176]{2,1,0:T(8,128)(2,1)S(1)}, u32[]{:S(2)}) copy-start(bf16[4,80,2176]{2,1,0:T(8,128)(2,1)S(1)} %all_to_all.20.rows_ref) | copy-start | bytes 4177924
  58.3 7.4 %copy-start.1 = (bf16[4,64,2176]{2,1,0:T(8,128)(2,1)}, bf16[4,64,2176]{2,1,0:T(8,128)(2,1)S(1)}, u32[]{:S(2)}) copy-start(bf16[4,64,2176]{2,1,0:T(8,128)(2,1)S(1)} %all_to_all.21.near_ref) | copy-start | bytes 3342340
  58.3 7.3 %collective-permute-start = (bf16[4,64,2176]{2,1,0:T(8,128)(2,1)S(1)}, bf16[4,64,2176]{2,1,0:T(8,128)(2,1)}, u32[]{:S(2)}, u32[]{:S(2)}) collective-permute-start(bf16[4,64,2176]{2,1,0:T(8,128)(2,1)S(1)} %all_to_all.21.near_ref), channel_id=1, source_target_pairs={{0,1},{1,0},{2,3},{3,2},{4,5},{5,4},{6,7},{7,6},{8,9},{9,8},{10,11... | collective-permute-start | bytes 3342344 | tf_op jit(solution)/shard_map/ppermute | solution.py:233
  71.3 37.7 %all-to-all-start.2 = ((f32[16,32,256]{2,1,0:T(8,128)}), f32[16,32,256]{2,1,0:T(8,128)S(1)}, u32[]{:S(2)}, u32[]{:S(2)}) async-start(f32[16,32,256]{2,1,0:T(8,128)} %bitcast.22), calls=%async_computation.2 | async-start | bytes 1048576 | tf_op jit(solution)/shard_map/all_to_all | solution.py:245
  109.0 0.8 copy-start.3

commit v2 on v1

v2 whole, which is shorter than its diff:
```python
import jax
import jax.numpy as jnp
from jax import lax
from jax.experimental import pallas as pl
from jax.experimental.pallas import tpu as pltpu
from jax.sharding import PartitionSpec as P

F32 = jnp.float32
BF16 = jnp.bfloat16
NB = 64
CHUNKS = 17
WIDTH = CHUNKS * 128
ROWS = 64
SIDE = 4
DEPTH = 80
SLAB = 72
PAIRS = 16
VMEM = pl.BlockSpec(memory_space=pltpu.VMEM)
SMEM = pl.BlockSpec(memory_space=pltpu.SMEM)


def iota(shape, dim):
    return lax.broadcasted_iota(jnp.int32, shape, dim)


def ones_where(cond, dtype=F32):
    return jnp.where(cond, 1.0, 0.0).astype(dtype)


def nt(a, b, precision=None):
    return lax.dot_general(a, b, (((1,), (1,)), ((), ())), precision=precision, preferred_element_type=F32)


def tn(a, b, precision=None):
    return lax.dot_general(a, b, (((0,), (0,)), ((), ())), precision=precision, preferred_element_type=F32)


def nn(a, b, precision=None):
    return lax.dot_general(a, b, (((1,), (0,)), ((), ())), precision=precision, preferred_element_type=F32)


def thirds(x):
    high = x.astype(BF16)
    rest = x - high.astype(F32)
    middle = rest.astype(BF16)
    return high, middle, (rest - middle.astype(F32)).astype(BF16)


def folded(read, weigh):
    lane = iota((ROWS, 128), 1)
    column = lane & (NB - 1)
    chunks = []
    spill = jnp.zeros((ROWS, 128), F32)
    for q in range(16):
        low = read(q)
        high = read(31 - q)
        if weigh:
            low = jnp.where((column >> 1) == q, low * 0.5, low)
        turned = pltpu.roll(high, 2 * q, 1) if q else high
        chunks.append(jnp.where(column >= 2 * q, low, turned))
        block = (column >> 1) == (31 - q)
        spill = jnp.where(block, high * 0.5 if weigh else high, spill)
    return chunks, spill


def products(kind_ref, class_ref, x_ref, z_ref, tile_ref, both_ref, left_ref, right_ref, turned_ref):
    s = iota((NB, NB), 0)
    turn = ones_where(iota((NB, NB), 1) == ((s & 31) * 2 + (s >> 5)), BF16)
    rr = iota((NB, NB), 0)
    cc = iota((NB, NB), 1)
    empty = jnp.zeros((NB, NB), BF16)

    def beside(u, v):
        return jnp.concatenate([u, v], axis=1)

    for k in range(x_ref.shape[0]):
        active = (NB // 2) * (1 + class_ref[k])
        inside = (rr < active) & (cc < active)
        x = jnp.where(inside, x_ref[k].astype(F32), 0.0).astype(BF16)
        z = jnp.where(inside, z_ref[k].astype(F32), 0.0).astype(BF16)
        half = nt(x, turn).astype(BF16)
        full = nn(turn, half).astype(BF16)
        left_ref[k, 0:NB, :] = beside(full, full)
        left_ref[k, NB : 2 * NB, :] = beside(half, half)
        right_ref[k, 0:NB, :] = beside(z, empty)
        right_ref[k, NB : 2 * NB, :] = beside(empty, z)
        back = nn(turn, z).astype(BF16)
        turned_ref[k] = beside(back, back)

    def first(rows):
        return iota((rows, 128), 1) < NB

    def split(v):
        none = jnp.zeros_like(v)
        low = first(v.shape[0])
        return jnp.concatenate([jnp.where(low, v, none), jnp.where(low, none, v)], axis=0)

    def step(outer, carry):
        for inner in range(PAIRS):
            i = (outer * PAIRS + inner) * 2
            k0 = kind_ref[0, i]
            k1 = kind_ref[0, i + 1]
            at0 = pl.ds(pl.multiple_of(i * 32, 32), 32)
            at1 = pl.ds(pl.multiple_of(i * 32 + 32, 32), 32)
            tile0 = tile_ref[pl.ds(i, 32, stride=ROWS), :]
            tile1 = tile_ref[pl.ds(i + 1, 32, stride=ROWS), :]
            low = first(32)
            top = jnp.where(low, tile0, pltpu.roll(tile1, NB, 1))
            bottom = jnp.where(low, pltpu.roll(tile0, NB, 1), tile1)
            pieces = split(jnp.concatenate([top, bottom], axis=0)).astype(BF16)
            left = nn(jnp.where(first(2 * NB), left_ref[k0], left_ref[k1]), pieces)
            right = jnp.concatenate([right_ref[k0, 0:NB, :], right_ref[k1, NB : 2 * NB, :]], axis=0)
            turned = jnp.where(first(NB), turned_ref[k0], turned_ref[k1])
            both = nn(left[:NB].astype(BF16), right) + nt(turned, split(left[NB:]).astype(BF16))
            top = both[:32]
            bottom = both[32:]
            both_ref[at0, :] = jnp.where(low, top, pltpu.roll(bottom, NB, 1))
            both_ref[at1, :] = jnp.where(low, pltpu.roll(top, NB, 1), bottom)
        return carry

    lax.fori_loop(0, ROWS // (2 * PAIRS), step, 0)


def pack_kernel(
    kind_ref, class_ref, a_ref, x_ref, z_ref, slot_ref, touched_ref, out_ref, tile_ref, both_ref, left_ref, right_ref, turned_ref
):
    for q in range(32):
        tile_ref[q * ROWS : (q + 1) * ROWS, :] = a_ref[:, q * 128 : (q + 1) * 128].astype(F32)
    products(kind_ref, class_ref, x_ref, z_ref, tile_ref, both_ref, left_ref, right_ref, turned_ref)
    r = iota((ROWS, ROWS), 0)
    c = iota((ROWS, ROWS), 1)

    def as_column(row):
        return jnp.sum(jnp.where(r == c, row, 0.0), axis=1, keepdims=True)

    slot = slot_ref[...]
    owner_row = (slot >> 6).astype(F32)
    inner_row = (slot & (ROWS - 1)).astype(F32)
    touched_row = touched_ref[...].astype(F32)
    owner_full = jnp.broadcast_to(owner_row, (ROWS, ROWS))
    owner_col = as_column(owner_full)
    inner_col = as_column(jnp.broadcast_to(inner_row, (ROWS, ROWS)))
    touched_col = as_column(jnp.broadcast_to(touched_row, (ROWS, ROWS)))
    rank = jnp.sum(ones_where((owner_col == owner_full) & (r < c)), axis=0, keepdims=True)
    lower = jnp.sum(ones_where(owner_col < owner_full), axis=0, keepdims=True)
    place = rank * 16.0 + lower * 0.25
    select = ones_where(r.astype(F32) == place, BF16)
    lane = iota((ROWS, 128), 1)

    def with_ids(spill, first):
        ids = jnp.where(lane == first, touched_col, jnp.where(lane == first + 1, owner_col, inner_col))
        return jnp.where((lane & (NB - 1)) >= 32, spill, jnp.where((lane >= first) & (lane < first + 3), ids, 0.0))

    chunks, spill = folded(lambda q: a_ref[:, q * 128 : (q + 1) * 128].astype(F32), False)
    chunks.append(with_ids(spill, 0))
    for q, chunk in enumerate(chunks):
        picked = nn(select, chunk.astype(BF16)).astype(BF16)
        for k in range(SIDE):
            out_ref[k, 0:16, q * 128 : (q + 1) * 128] = picked[16 * k : 16 * (k + 1)]
    chunks, spill = folded(lambda q: both_ref[pl.ds(q, ROWS, stride=32), :], True)
    chunks.append(with_ids(spill, 3))
    for q, chunk in enumerate(chunks):
        rounded = chunk.astype(BF16)
        for k in range(SIDE):
            out_ref[k, 16:80, q * 128 : (q + 1) * 128] = rounded


def near_kernel(rows_ref, near_ref, score_ref, col_id_ref, row_id_ref, row_ref):
    rows = jnp.concatenate([rows_ref[k, 16:80, :] for k in range(SIDE)], axis=0)
    near = near_ref[...].reshape(256, WIDTH)
    score_ref[...] = nt(near, rows)
    row_ids = rows[:, 16 * 128 :]
    col_id_ref[...] = near[:, 16 * 128 :]
    row_id_ref[...] = row_ids
    row_t = nt(ones_where(iota((8, 128), 0) + 3 == iota((8, 128), 1), BF16), row_ids)
    lane = iota((256, 128), 1).astype(F32)
    own = ones_where(row_ids.astype(F32)[:, 4:5] == lane, BF16)
    i = iota((256, 256), 0)
    j = iota((256, 256), 1)
    rank = jnp.sum(jnp.where((i < j) & ((i >> 6) == (j >> 6)), nt(own, own), 0.0), axis=0, keepdims=True)
    line = (iota((1, 256), 1) >> 6).astype(F32)
    row_ref[0:1, :] = row_t[1:2, :] * 8.0 + line
    row_ref[1:2, :] = rank
    row_ref[2:3, :] = row_t[2:3, :] + 1.0
    row_ref[3:8, :] = jnp.zeros((5, 256), F32)


def score_kernel(core_ref, rows_ref, far_ref, score_ref, col_id_ref, row_id_ref, out_ref, col_ref):
    n_rows, n_cols = 256, 512
    rows = jnp.concatenate([rows_ref[k, 16:80, :] for k in range(SIDE)], axis=0)
    far = far_ref[...].reshape(256, WIDTH)
    scores = jnp.concatenate([score_ref[...], nt(far, rows)], axis=0)
    col_ids = jnp.concatenate([col_id_ref[...], far[:, 16 * 128 :]], axis=0)
    col_t = nt(ones_where(iota((8, 128), 0) == iota((8, 128), 1), BF16), col_ids)
    lane_c = iota((n_cols, 128), 1).astype(F32)
    lane_r = iota((n_rows, 128), 1).astype(F32)
    col_f = col_ids.astype(F32)
    kind_c = ones_where(col_f[:, 0:1] == lane_c, BF16)
    kind_r = ones_where(row_id_ref[...].astype(F32)[:, 3:4] == lane_r, BF16)
    scores = jnp.where(nt(kind_c, kind_r) > 0.5, scores, 0.0)
    own_c = ones_where(col_f[:, 1:2] == lane_c, BF16)
    i = iota((n_cols, n_cols), 0)
    j = iota((n_cols, n_cols), 1)
    turn = core_ref[0] * 256
    rank = jnp.sum(jnp.where((i ^ turn) < (j ^ turn), nt(own_c, own_c), 0.0), axis=0, keepdims=True)
    move = ones_where(i.astype(F32) == col_t[1:2, :] * 16.0 + rank, BF16)
    top = jnp.max(jnp.max(jnp.abs(scores), axis=0, keepdims=True), axis=1, keepdims=True)
    power = jnp.ceil(jnp.log(jnp.maximum(top, 1e-36)) * 1.4426950408889634)
    scaled = scores * jnp.exp2(-power)
    high = scaled.astype(BF16)
    low = (scaled - high.astype(F32)).astype(BF16)
    moved = nn(move, high) + nn(move, low)
    note = jnp.broadcast_to(power, (8, 128))
    for g in range(16):
        out_ref[g, 0:32, :] = moved[32 * g : 32 * (g + 1), 0:128]
        out_ref[g, 32:64, :] = moved[32 * g : 32 * (g + 1), 128:256]
        out_ref[g, 64:72, :] = note
    odd = col_t[1:2, :] - 2.0 * jnp.floor(col_t[1:2, :] * 0.5)
    col_id = (odd * 64.0 + col_t[2:3, :]).astype(BF16)
    col_ref[...] = nt(jnp.broadcast_to(col_id, (8, n_cols)), move)


def send_kernel(group_ref, total_ref, col_ref, row_ref, out_ref):
    total = jnp.concatenate([total_ref[0:32, :], total_ref[32:64, :]], axis=1)
    target = row_ref[0:1, :]
    rank = row_ref[1:2, :]
    m = iota((256, 256), 0).astype(F32)
    hit = (m == target) | (m == target + 4.0)
    pick = jnp.concatenate([ones_where(hit & (rank == float(k)), BF16) for k in range(SIDE)], axis=0)
    high, middle, low = thirds(total)
    inner = jnp.broadcast_to(row_ref[2:3, :], (16, 256)).astype(BF16)
    found = nt(pick, jnp.concatenate([high, inner], axis=0))
    value = found[:, 0:32] + (nt(pick, middle) + nt(pick, low))
    index = jnp.broadcast_to(found[:, 32:33], (4 * 256, 32))
    s = iota((512, 128), 0)
    lane = iota((512, 128), 1)
    here = ones_where(s == group_ref[0] * 32 + (lane & 31), BF16)
    cols = nn(col_ref[...].astype(BF16), here)[0:1, :]
    values = jnp.concatenate([value[256 * k : 256 * (k + 1)] for k in range(SIDE)], axis=1)
    indices = jnp.concatenate([index[256 * k : 256 * (k + 1)] for k in range(SIDE)], axis=1)
    is_id = (iota((256, 128), 0) & 7) >= 4
    out_ref[...] = jnp.where(is_id, indices * 128.0 + cols, values)


def land_kernel(in_ref, out_ref):
    wide = jnp.concatenate([in_ref[64 * x : 64 * (x + 1), :] for x in range(SIDE)], axis=1)
    lane = (iota((64, 512), 1) >> 5) & 3
    index = in_ref[0:64, :]
    high = pltpu.roll(jnp.floor(index * (1.0 / 128.0)), 60, 0)
    is_value = (iota((64, 64), 0) & 7) < 4
    spot = iota((64, 64), 1).astype(F32) + 1.0
    place = jnp.concatenate(
        [ones_where(is_value & (high[:, 32 * k : 32 * k + 1] == spot), BF16) for k in range(SIDE)], axis=0
    )
    own = [jnp.where(lane == k, wide, 0.0) for k in range(SIDE)]
    total = None
    for part in thirds(jnp.concatenate(own, axis=0)):
        term = tn(place, part)
        total = term if total is None else total + term
    id_row = wide[4:5, :]
    col = id_row - 128.0 * jnp.floor(id_row * (1.0 / 128.0))
    spread = ones_where(iota((128, 512), 0).astype(F32) == col, BF16)
    high, middle, low = thirds(total)
    out_ref[...] = nt(high, spread) + (nt(middle, spread) + nt(low, spread))


def near_by(*dims, dtype=F32):
    return pltpu.VMEM(dims, dtype)


def shape(*dims, dtype=F32):
    return jax.ShapeDtypeStruct(dims, dtype)


def call(kernel, out, n, scalars=0, scratch=(), held=()):
    many = isinstance(out, tuple)
    run = pl.pallas_call(
        kernel,
        out_shape=out,
        in_specs=[SMEM] * scalars + [VMEM] * (n - scalars),
        out_specs=tuple(VMEM for _ in out) if many else VMEM,
        scratch_shapes=list(scratch),
    )

    def placed(*args):
        return run(
            *(pltpu.with_memory_space_constraint(a, pltpu.VMEM) if i in held else a for i, a in enumerate(args))
        )

    return placed


def device(x, y, c):
    return (x * SIDE + y) * 2 + c


LINES_X = [[device(x, y, c) for x in range(SIDE)] for y in range(SIDE) for c in range(2)]
LINES_Y = [[device(x, y, c) for y in range(SIDE)] for x in range(SIDE) for c in range(2)]
SWAP = [(device(x, y, c), device(x, y, 1 - c)) for x in range(SIDE) for y in range(SIDE) for c in range(2)]


def shards(a_pieces, touched, slot_row, x_blocks, z_inverse, block_class):
    blocks = x_blocks.shape[0]
    packed = call(
        pack_kernel,
        near_by(SIDE, DEPTH, WIDTH, dtype=BF16),
        7,
        2,
        (
            pltpu.VMEM((ROWS * 32, 128), F32),
            pltpu.VMEM((ROWS * 32, 128), F32),
            pltpu.VMEM((blocks, 2 * NB, 2 * NB), BF16),
            pltpu.VMEM((blocks, 2 * NB, 2 * NB), BF16),
            pltpu.VMEM((blocks, NB, 2 * NB), BF16),
        ),
    )(touched, block_class, a_pieces[0], x_blocks, z_inverse, slot_row[None, :], touched)
    lined = lax.all_to_all(packed, "row", 0, 0, tiled=True, axis_index_groups=LINES_X)
    mine = lined[:, :16, :].reshape(ROWS, WIDTH)
    near = lax.all_to_all(
        jnp.broadcast_to(mine[None], (SIDE, ROWS, WIDTH)), "row", 0, 0, tiled=True, axis_index_groups=LINES_Y
    )
    far = lax.ppermute(near, "row", SWAP)
    near_scores, col_ids, row_ids, rows = call(
        near_kernel, (shape(256, 256), shape(256, 128, dtype=BF16), shape(256, 128, dtype=BF16), shape(8, 256)), 2
    )(lined, near)
    core = (lax.axis_index("row").astype(jnp.int32) & 1).reshape(1)
    scores, cols = call(score_kernel, (near_by(16, SLAB, 128), near_by(8, 512)), 6, 1, held=())(
        core, lined, far, near_scores, col_ids, row_ids
    )
    group = lax.axis_index("grp").astype(jnp.int32).reshape(1)
    sent, cols, rows, group = lax.optimization_barrier((scores.astype(jnp.float16), cols, rows, group))
    arrived = lax.all_to_all(sent, "grp", 0, 0, tiled=True).astype(F32)
    total = jnp.sum(arrived[:, :64] * jnp.exp2(arrived[:, 64:65]), axis=0)
    outgoing = call(send_kernel, near_by(256, 128), 4, 1, held=(1, 2))(group, total, cols, rows)
    incoming = lax.all_to_all(outgoing.reshape(32, 8, 128), "row", 0, 0, tiled=True)
    return call(land_kernel, shape(64, 128), 1, held=(0,))(incoming.reshape(256, 128))


def solution(mesh):
    return jax.shard_map(
        shards,
        mesh=mesh,
        in_specs=(
            P("grp", "row", None),
            P("grp", "row"),
            P("row"),
            P("grp", None, None),
            P("grp", None, None),
            P("grp"),
        ),
        out_specs=P("row", "grp"),
        check_vma=False,
    )
```

time: 136 us -> 108 us (0.79)
  blocking collectives: 59.6 us -> 86.3 us
  waiting for transfers between devices: 25.2 us -> 0.01 us
  starting transfers between devices: 19.8 us -> 4.84 us
  local copies, waits for them, and re-layouts: 8.94 us -> 0.11 us
  other arithmetic: 4.53 us -> 0.15 us
  matrix products: 2.25 us -> 0 us
    all_to_all x0 -> x1, blocking collectives: none -> 29.2 us  [shards(): arrived = lax.all_to_all(sent, 'grp', 0, 0, tiled=True).astype(F32)]
    all_to_all x1 -> x0, waiting for transfers between devices: 22.7 us -> none  [shards(): lax.all_to_all(scores.reshape(16, 32, 256), 'grp', 0, 0, tiled=True)]
    all_to_all x1 -> x0, starting transfers between devices: 14.9 us -> none  [shards(): lax.all_to_all(scores.reshape(16, 32, 256), 'grp', 0, 0, tiled=True)]
    ppermute x1, waiting for transfers between devices: 2.48 us -> 0.01 us  [shards(): far = lax.ppermute(near, 'row', SWAP)]
    all_to_all x1, blocking collectives: 19.1 us -> 16.7 us  [shards(): lax.all_to_all(outgoing.reshape(32, 8, 128), 'row', 0, 0, tiled=True)]
    gather x2 -> x0, local copies, waits for them, and re-layouts: 2.4 us -> none  [the longest x1 1.65 us: shards(): z_masked[own_block]]
    dot_general x1 -> x0, matrix products: 2.25 us -> none  [shards(): jnp.einsum('rab,rbc->rac', left, z_masked[own_block], preferred_element_t...]
    another operation x1 -> x0, local copies, waits for them, and re-layouts: 2.14 us -> none  [shards(): pieces = a_local.reshape(ROWS, NB, NB)]
  transfers between devices with their start and end apart: 2 -> 1, of which waited for: 2 -> 0; matrix products, arithmetic and copies ran while one was open for 0% -> 0% of each run, Pallas kernels for 0% -> 3%
where the time goes in v2:
time: 108 us; the launch traced here: 107 us
  blocking collectives  86.3 us (80%)
  Pallas kernels  15.7 us (15%)
  starting transfers between devices  4.84 us (4%)
    all_to_all x1, blocking collectives, shards(): arrived = lax.all_to_all(sent, 'grp', 0, 0, tiled=True).astype(F32)  29.2 us
    all_to_all x1, blocking collectives, shards(): lax.all_to_all(jnp.broadcast_to(mine[None], (SIDE, ROWS, WIDTH)), 'row',...  21.8 us
    all_to_all x1, blocking collectives, shards(): lax.all_to_all(packed, 'row', 0, 0, tiled=True, axis_index_groups=LINES_X)  18.6 us
    all_to_all x1, blocking collectives, shards(): lax.all_to_all(outgoing.reshape(32, 8, 128), 'row', 0, 0, tiled=True)  16.7 us
    pallas_call x5, Pallas kernels, placed(): run(*(pltpu.with_memory_space_constraint(a, pltpu.VMEM) if i in held else...  15.7 us
    ppermute x1, starting transfers between devices, shards(): far = lax.ppermute(near, 'row', SWAP)  4.84 us
  transfers between devices with their start and end apart: 1, of which 0 were waited for; matrix products, arithmetic and copies ran while one was open for 0% of the time, Pallas kernels for 3%

profile of v2, /device:TPU:1, one launch (start us, length us, event | category | flops | bytes accessed | tf_op | source)
XLA Modules:
  0.0 107.2 jit_solution(700059756754910516)
XLA Ops:
  0.0 6.6 %shard_map.64 = bf16[4,80,2176]{2,1,0:T(8,128)(2,1)S(1)} custom-call(s32[1,64]{1,0:T(1,128)} %touched_ref.1, s32[8]{0:T(128)} %class_ref.1, bf16[64,4096]{1,0:T(8,128)(2,1)} %bitcast.11, bf16[8,64,64]{2,1,0:T(8,128)(2,1)} %x_ref.1, bf16[8,64,64]{2,1,0:T(8,128)(2,1)} %z_ref.1, s32[1,64]{1,0:T(1,128)} %bitcast.13, s32[1,64]{1,0:T(1,128)} %touched_ref.1), custom_call_target="tpu_custom_call" | custom-call | tf_op jit(solution)/shard_map/pallas_call | solution.py:286
  6.6 18.6 %all_to_all.20.rows_ref = bf16[4,80,2176]{2,1,0:T(8,128)(2,1)S(1)} all-to-all(bf16[4,80,2176]{2,1,0:T(8,128)(2,1)S(1)} %shard_map.64), channel_id=1, replica_groups={{0,8,16,24},{1,9,17,25},{2,10,18,26},{3,11,19,27},{4,12,20,28},{5,13,21..., dimensions={0} | all-to-all | bytes 2785280 | tf_op jit(solution)/shard_map/all_to_all | solution.py:317
  25.2 0.0 copy-start
  25.3 0.1 broadcast_in_dim.12
  25.3 21.8 %all_to_all.21.near_ref = bf16[4,64,2176]{2,1,0:T(8,128)(2,1)S(1)} all-to-all(bf16[4,64,2176]{2,1,0:T(8,128)(2,1)S(1)} %broadcast_in_dim.12), channel_id=1, replica_groups={{0,2,4,6},{1,3,5,7},{8,10,12,14},{9,11,13,15},{16,18,20,22},{17,19,21,2..., dimensions={0} | all-to-all | bytes 2228224 | tf_op jit(solution)/shard_map/all_to_all | solution.py:319
  47.1 0.0 copy-done
  47.1 0.0 copy-start.1
  47.1 4.8 %collective-permute-start = (bf16[4,64,2176]{2,1,0:T(8,128)(2,1)S(1)}, bf16[4,64,2176]{2,1,0:T(8,128)(2,1)}, u32[]{:S(2)}, u32[]{:S(2)}) collective-permute-start(bf16[4,64,2176]{2,1,0:T(8,128)(2,1)S(1)} %all_to_all.21.near_ref), channel_id=1, source_target_pairs={{0,1},{1,0},{2,3},{3,2},{4,5},{5,4},{6,7},{7,6},{8,9},{9,8},{10,11... | collective-permute-start | bytes 3342344 | tf_op jit(solution)/shard_map/ppermute | solution.py:322
  52.0 0.0 copy-done.1
  52.0 2.9 %shard_map.65 = (f32[256,256]{1,0:T(8,128)}, bf16[256,128]{1,0:T(8,128)(2,1)}, bf16[256,128]{1,0:T(8,128)(2,1)}, f32[8,256]{1,0:T(8,128)}) custom-call(bf16[4,80,2176]{2,1,0:T(8,128)(2,1)} %copy-done, bf16[4,64,2176]{2,1,0:T(8,128)(2,1)} %copy-done.1), custom_call_target="tpu_custom_call" | custom-call | tf_op jit(solution)/shard_map/pallas_call | solution.py:286
  54.9 0.0 collective-permute-done.far_ref
  54.9 3.5 %shard_map.66 = (f32[16,72,128]{2,1,0:T(8,128)S(1)}, f32[8,512]{1,0:T(8,128)S(1)}) custom-call(s32[1]{0:T(128)} %bitcast.core_ref, bf16[4,80,2176]{2,1,0:T(8,128)(2,1)} %copy-done, bf16[4,64,2176]{2,1,0:T(8,128)(2,1)} %collective-permute-done.far_ref, f32[256,256]{1,0:T(8,128)} %get-tuple-element.15.score_ref, ...), custom_call_target="tpu_custom_call" | custom-call | tf_op jit(solution)/shard_map/pallas_call | solution.py:286
  58.4 29.2 %all_to_all.22 = f16[16,72,128]{2,1,0:T(8,128)(2,1)S(1)} all-to-all(f16[16,72,128]{2,1,0:T(8,128)(2,1)S(1)} %convert_element_type.6), channel_id=1, replica_groups=mesh['grp'=16,'row'=32] {'grp'}, dimensions={0} | all-to-all | bytes 589824 | tf_op jit(solution)/shard_map/all_to_all | solution.py:332
  87.7 0.1 fusion.total_ref
  87.8 1.4 %shard_map.67 = f32[256,128]{1,0:T(8,128)S(1)} custom-call(s32[1]{0:T(128)} %bitcast.4.group_ref, f32[64,128]{1,0:T(8,128)S(1)} %fusion.total_ref, f32[8,512]{1,0:T(8,128)S(1)} %get-tuple-element.23.col_ref, f32[8,256]{1,0:T(8,128)} %get-tuple-element.24.row_ref), custom_call_target="tpu_custom_call" | custom-call | tf_op jit(solution)/shard_map/pallas_call | solution.py:286
  89.1 16.7 %all_to_all.23 = f32[32,8,128]{2,1,0:T(8,128)S(1)} all-to-all(f32[32,8,128]{2,1,0:T(8,128)S(1)} %bitcast.9), channel_id=1, replica_groups=mesh['grp'=16,'row'=32] {'row'}, dimensions={0} | all-to-all | bytes 262144 | tf_op jit(solution)/shard_map/all_to_all | solution.py:335
  105.8 1.3 %shard_map.68 = f32[64,128]{1,0:T(8,128)} custom-call(f32[256,128]{1,0:T(8,128)S(1)} %bitcast.8), custom_call_target="tpu_custom_call" | custom-call | tf_op jit(solution)/shard_map/pallas_call | solution.py:286
  (4 shorter events, 0.1 us)
Async XLA Ops:
  25.2 21.9 %copy-start = (bf16[4,80,2176]{2,1,0:T(8,128)(2,1)}, bf16[4,80,2176]{2,1,0:T(8,128)(2,1)S(1)}, u32[]{:S(2)}) copy-start(bf16[4,80,2176]{2,1,0:T(8,128)(2,1)S(1)} %all_to_all.20.rows_ref) | copy-start | bytes 4177924
  47.1 4.9 %copy-start.1 = (bf16[4,64,2176]{2,1,0:T(8,128)(2,1)}, bf16[4,64,2176]{2,1,0:T(8,128)(2,1)S(1)}, u32[]{:S(2)}) copy-start(bf16[4,64,2176]{2,1,0:T(8,128)(2,1)S(1)} %all_to_all.21.near_ref) | copy-start | bytes 3342340
  47.1 7.8 %collective-permute-start = (bf16[4,64,2176]{2,1,0:T(8,128)(2,1)S(1)}, bf16[4,64,2176]{2,1,0:T(8,128)(2,1)}, u32[]{:S(2)}, u32[]{:S(2)}) collective-permute-start(bf16[4,64,2176]{2,1,0:T(8,128)(2,1)S(1)} %all_to_all.21.near_ref), channel_id=1, source_target_pairs={{0,1},{1,0},{2,3},{3,2},{4,5},{5,4},{6,7},{7,6},{8,9},{9,8},{10,11... | collective-permute-start | bytes 3342344 | tf_op jit(solution)/shard_map/ppermute | solution.py:322

commit v3 on v2

--- a/solution.py
+++ b/solution.py
@@ -12,9 +12,10 @@
 WIDTH = CHUNKS * 128
 ROWS = 64
 SIDE = 4
-DEPTH = 80
 SLAB = 72
-PAIRS = 16
+QUADS = 8
+GRANT = 16 << 20
+WIDE = 60 << 20
 VMEM = pl.BlockSpec(memory_space=pltpu.VMEM)
 SMEM = pl.BlockSpec(memory_space=pltpu.SMEM)
 
@@ -95,115 +96,121 @@
         low = first(v.shape[0])
         return jnp.concatenate([jnp.where(low, v, none), jnp.where(low, none, v)], axis=0)
 
+    def corners(u, v):
+        none = jnp.zeros_like(u)
+        return jnp.concatenate([beside(u, none), beside(none, v)], axis=0)
+
     def step(outer, carry):
-        for inner in range(PAIRS):
-            i = (outer * PAIRS + inner) * 2
-            k0 = kind_ref[0, i]
-            k1 = kind_ref[0, i + 1]
-            at0 = pl.ds(pl.multiple_of(i * 32, 32), 32)
-            at1 = pl.ds(pl.multiple_of(i * 32 + 32, 32), 32)
-            tile0 = tile_ref[pl.ds(i, 32, stride=ROWS), :]
-            tile1 = tile_ref[pl.ds(i + 1, 32, stride=ROWS), :]
-            low = first(32)
-            top = jnp.where(low, tile0, pltpu.roll(tile1, NB, 1))
-            bottom = jnp.where(low, pltpu.roll(tile0, NB, 1), tile1)
-            pieces = split(jnp.concatenate([top, bottom], axis=0)).astype(BF16)
-            left = nn(jnp.where(first(2 * NB), left_ref[k0], left_ref[k1]), pieces)
-            right = jnp.concatenate([right_ref[k0, 0:NB, :], right_ref[k1, NB : 2 * NB, :]], axis=0)
-            turned = jnp.where(first(NB), turned_ref[k0], turned_ref[k1])
-            both = nn(left[:NB].astype(BF16), right) + nt(turned, split(left[NB:]).astype(BF16))
-            top = both[:32]
-            bottom = both[32:]
-            both_ref[at0, :] = jnp.where(low, top, pltpu.roll(bottom, NB, 1))
-            both_ref[at1, :] = jnp.where(low, pltpu.roll(top, NB, 1), bottom)
+        low = first(32)
+        for inner in range(QUADS):
+            i = (outer * QUADS + inner) * 4
+            k = [kind_ref[0, i + n] for n in range(4)]
+            cats, lefts, rights, backs = [], [], [], []
+            for p in (0, 2):
+                tile0 = tile_ref[pl.ds(i + p, 32, stride=ROWS), :]
+                tile1 = tile_ref[pl.ds(i + p + 1, 32, stride=ROWS), :]
+                top = jnp.where(low, tile0, pltpu.roll(tile1, NB, 1))
+                bottom = jnp.where(low, pltpu.roll(tile0, NB, 1), tile1)
+                cats.append(split(jnp.concatenate([top, bottom], axis=0)).astype(BF16))
+                lefts.append(jnp.where(first(2 * NB), left_ref[k[p]], left_ref[k[p + 1]]))
+                rights.append(
+                    jnp.concatenate([right_ref[k[p], 0:NB, :], right_ref[k[p + 1], NB : 2 * NB, :]], axis=0)
+                )
+                backs.append(jnp.where(first(NB), turned_ref[k[p]], turned_ref[k[p + 1]]))
+            left = nn(beside(*lefts), corners(*cats))
+            halves = [split(left[NB:, 128 * p : 128 * (p + 1)]).astype(BF16) for p in range(2)]
+            both = nn(left[:NB].astype(BF16), corners(*rights)) + nt(beside(*backs), corners(*halves))
+            for p in range(2):
+                top = both[:32, 128 * p : 128 * (p + 1)]
+                bottom = both[32:, 128 * p : 128 * (p + 1)]
+                at = pl.multiple_of((i + 2 * p) * 32, 64)
+                both_ref[pl.ds(at, 32), :] = jnp.where(low, top, pltpu.roll(bottom, NB, 1))
+                both_ref[pl.ds(at + 32, 32), :] = jnp.where(low, pltpu.roll(top, NB, 1), bottom)
         return carry
 
-    lax.fori_loop(0, ROWS // (2 * PAIRS), step, 0)
-
-
-def pack_kernel(
-    kind_ref, class_ref, a_ref, x_ref, z_ref, slot_ref, touched_ref, out_ref, tile_ref, both_ref, left_ref, right_ref, turned_ref
+    lax.fori_loop(0, ROWS // (4 * QUADS), step, 0)
+
+
+def slot_table(me_ref, slot_ref, touched_ref):
+    r = iota((ROWS, ROWS), 0)
+    c = iota((ROWS, ROWS), 1)
+
+    def spread(row):
+        full = jnp.broadcast_to(row, (ROWS, ROWS))
+        return full, jnp.sum(jnp.where(r == c, full, 0.0), axis=1, keepdims=True)
+
+    slot = slot_ref[...]
+    owner_full, owner_col = spread((slot >> 6).astype(F32))
+    _, inner_col = spread((slot & (ROWS - 1)).astype(F32))
+    _, touched_col = spread(touched_ref[...].astype(F32))
+    rank = jnp.sum(ones_where((owner_col == owner_full) & (r < c)), axis=0, keepdims=True)
+    lower = jnp.sum(ones_where(owner_col < owner_full), axis=0, keepdims=True)
+    holder = jnp.full((ROWS, 1), me_ref[0], jnp.int32).astype(F32)
+    return (touched_col, owner_col, inner_col, holder), rank * 16.0 + lower * 0.25
+
+
+def with_ids(spill, columns, first):
+    lane = iota((ROWS, 128), 1)
+    ids = jnp.zeros((ROWS, 128), F32)
+    for n, column in enumerate(columns):
+        ids = jnp.where(lane == first + n, column, ids)
+    return jnp.where((lane & (NB - 1)) >= 32, spill, ids)
+
+
+def pack_kernel(me_ref, a_ref, slot_ref, touched_ref, out_ref):
+    columns, place = slot_table(me_ref, slot_ref, touched_ref)
+    select = ones_where(iota((ROWS, ROWS), 0).astype(F32) == place, BF16)
+    chunks, spill = folded(lambda q: a_ref[:, q * 128 : (q + 1) * 128].astype(F32), False)
+    chunks.append(with_ids(spill, columns, 0))
+    for q, chunk in enumerate(chunks):
+        picked = nn(select, chunk.astype(BF16)).astype(BF16)
+        for k in range(SIDE):
+            out_ref[k, :, q * 128 : (q + 1) * 128] = picked[16 * k : 16 * (k + 1)]
+
+
+def product_kernel(
+    me_ref, kind_ref, class_ref, a_ref, x_ref, z_ref, slot_ref, touched_ref, out_ref, tile_ref, both_ref, left_ref, right_ref, turned_ref
 ):
     for q in range(32):
         tile_ref[q * ROWS : (q + 1) * ROWS, :] = a_ref[:, q * 128 : (q + 1) * 128].astype(F32)
     products(kind_ref, class_ref, x_ref, z_ref, tile_ref, both_ref, left_ref, right_ref, turned_ref)
-    r = iota((ROWS, ROWS), 0)
-    c = iota((ROWS, ROWS), 1)
-
-    def as_column(row):
-        return jnp.sum(jnp.where(r == c, row, 0.0), axis=1, keepdims=True)
-
-    slot = slot_ref[...]
-    owner_row = (slot >> 6).astype(F32)
-    inner_row = (slot & (ROWS - 1)).astype(F32)
-    touched_row = touched_ref[...].astype(F32)
-    owner_full = jnp.broadcast_to(owner_row, (ROWS, ROWS))
-    owner_col = as_column(owner_full)
-    inner_col = as_column(jnp.broadcast_to(inner_row, (ROWS, ROWS)))
-    touched_col = as_column(jnp.broadcast_to(touched_row, (ROWS, ROWS)))
-    rank = jnp.sum(ones_where((owner_col == owner_full) & (r < c)), axis=0, keepdims=True)
-    lower = jnp.sum(ones_where(owner_col < owner_full), axis=0, keepdims=True)
-    place = rank * 16.0 + lower * 0.25
-    select = ones_where(r.astype(F32) == place, BF16)
-    lane = iota((ROWS, 128), 1)
-
-    def with_ids(spill, first):
-        ids = jnp.where(lane == first, touched_col, jnp.where(lane == first + 1, owner_col, inner_col))
-        return jnp.where((lane & (NB - 1)) >= 32, spill, jnp.where((lane >= first) & (lane < first + 3), ids, 0.0))
-
-    chunks, spill = folded(lambda q: a_ref[:, q * 128 : (q + 1) * 128].astype(F32), False)
-    chunks.append(with_ids(spill, 0))
-    for q, chunk in enumerate(chunks):
-        picked = nn(select, chunk.astype(BF16)).astype(BF16)
-        for k in range(SIDE):
-            out_ref[k, 0:16, q * 128 : (q + 1) * 128] = picked[16 * k : 16 * (k + 1)]
+    columns, _ = slot_table(me_ref, slot_ref, touched_ref)
     chunks, spill = folded(lambda q: both_ref[pl.ds(q, ROWS, stride=32), :], True)
-    chunks.append(with_ids(spill, 3))
+    chunks.append(with_ids(spill, columns, 4))
     for q, chunk in enumerate(chunks):
         rounded = chunk.astype(BF16)
         for k in range(SIDE):
-            out_ref[k, 16:80, q * 128 : (q + 1) * 128] = rounded
-
-
-def near_kernel(rows_ref, near_ref, score_ref, col_id_ref, row_id_ref, row_ref):
-    rows = jnp.concatenate([rows_ref[k, 16:80, :] for k in range(SIDE)], axis=0)
+            out_ref[k, :, q * 128 : (q + 1) * 128] = rounded
+
+
+def score_kernel(rows_ref, near_ref, far_ref, out_ref, col_ref, row_ref):
+    n_rows, n_cols = 256, 512
+    rows = rows_ref[...].reshape(n_rows, WIDTH)
     near = near_ref[...].reshape(256, WIDTH)
-    score_ref[...] = nt(near, rows)
+    far = far_ref[...].reshape(256, WIDTH)
+    scores = jnp.concatenate([nt(near, rows), nt(far, rows)], axis=0)
+    col_ids = jnp.concatenate([near[:, 16 * 128 :], far[:, 16 * 128 :]], axis=0)
     row_ids = rows[:, 16 * 128 :]
-    col_id_ref[...] = near[:, 16 * 128 :]
-    row_id_ref[...] = row_ids
-    row_t = nt(ones_where(iota((8, 128), 0) + 3 == iota((8, 128), 1), BF16), row_ids)
-    lane = iota((256, 128), 1).astype(F32)
-    own = ones_where(row_ids.astype(F32)[:, 4:5] == lane, BF16)
-    i = iota((256, 256), 0)
-    j = iota((256, 256), 1)
-    rank = jnp.sum(jnp.where((i < j) & ((i >> 6) == (j >> 6)), nt(own, own), 0.0), axis=0, keepdims=True)
-    line = (iota((1, 256), 1) >> 6).astype(F32)
-    row_ref[0:1, :] = row_t[1:2, :] * 8.0 + line
-    row_ref[1:2, :] = rank
+    pick = iota((8, 128), 0)
+    spot = iota((8, 128), 1)
+    col_t = nt(ones_where(pick == spot, BF16), col_ids)
+    row_t = nt(ones_where(pick + 4 == spot, BF16), row_ids)
+    col_f = col_ids.astype(F32)
+    row_f = row_ids.astype(F32)
+    lane_r = iota((n_rows, 128), 1).astype(F32)
+    own_r = ones_where(row_f[:, 5:6] == lane_r, BF16)
+    before = (iota((n_rows, n_rows), 0) < iota((n_rows, n_rows), 1)) & (row_f[:, 7:8] == row_t[3:4, :])
+    row_rank = jnp.sum(jnp.where(before, nt(own_r, own_r), 0.0), axis=0, keepdims=True)
+    row_ref[0:1, :] = row_t[1:2, :] * 8.0 + jnp.floor(row_t[3:4, :] * 0.125)
+    row_ref[1:2, :] = row_rank
     row_ref[2:3, :] = row_t[2:3, :] + 1.0
-    row_ref[3:8, :] = jnp.zeros((5, 256), F32)
-
-
-def score_kernel(core_ref, rows_ref, far_ref, score_ref, col_id_ref, row_id_ref, out_ref, col_ref):
-    n_rows, n_cols = 256, 512
-    rows = jnp.concatenate([rows_ref[k, 16:80, :] for k in range(SIDE)], axis=0)
-    far = far_ref[...].reshape(256, WIDTH)
-    scores = jnp.concatenate([score_ref[...], nt(far, rows)], axis=0)
-    col_ids = jnp.concatenate([col_id_ref[...], far[:, 16 * 128 :]], axis=0)
-    col_t = nt(ones_where(iota((8, 128), 0) == iota((8, 128), 1), BF16), col_ids)
+    row_ref[3:8, :] = jnp.zeros((5, n_rows), F32)
+    scores = jnp.where(col_f[:, 0:1] == row_t[0:1, :], scores, 0.0)
     lane_c = iota((n_cols, 128), 1).astype(F32)
-    lane_r = iota((n_rows, 128), 1).astype(F32)
-    col_f = col_ids.astype(F32)
-    kind_c = ones_where(col_f[:, 0:1] == lane_c, BF16)
-    kind_r = ones_where(row_id_ref[...].astype(F32)[:, 3:4] == lane_r, BF16)
-    scores = jnp.where(nt(kind_c, kind_r) > 0.5, scores, 0.0)
     own_c = ones_where(col_f[:, 1:2] == lane_c, BF16)
-    i = iota((n_cols, n_cols), 0)
-    j = iota((n_cols, n_cols), 1)
-    turn = core_ref[0] * 256
-    rank = jnp.sum(jnp.where((i ^ turn) < (j ^ turn), nt(own_c, own_c), 0.0), axis=0, keepdims=True)
-    move = ones_where(i.astype(F32) == col_t[1:2, :] * 16.0 + rank, BF16)
+    rank = jnp.sum(jnp.where(col_f[:, 3:4] < col_t[3:4, :], nt(own_c, own_c), 0.0), axis=0, keepdims=True)
+    place = col_t[1:2, :] * 16.0 + rank
+    move = ones_where(iota((n_cols, n_cols), 0).astype(F32) == place, BF16)
     top = jnp.max(jnp.max(jnp.abs(scores), axis=0, keepdims=True), axis=1, keepdims=True)
     power = jnp.ceil(jnp.log(jnp.maximum(top, 1e-36)) * 1.4426950408889634)
     scaled = scores * jnp.exp2(-power)
@@ -272,7 +279,7 @@
     return jax.ShapeDtypeStruct(dims, dtype)
 
 
-def call(kernel, out, n, scalars=0, scratch=(), held=()):
+def call(kernel, out, n, scalars=0, scratch=(), held=(), grant=GRANT):
     many = isinstance(out, tuple)
     run = pl.pallas_call(
         kernel,
@@ -280,6 +287,7 @@
         in_specs=[SMEM] * scalars + [VMEM] * (n - scalars),
         out_specs=tuple(VMEM for _ in out) if many else VMEM,
         scratch_shapes=list(scratch),
+        compiler_params=pltpu.CompilerParams(vmem_limit_bytes=grant),
     )
 
     def placed(*args):
@@ -295,17 +303,30 @@
 
 
 LINES_X = [[device(x, y, c) for x in range(SIDE)] for y in range(SIDE) for c in range(2)]
-LINES_Y = [[device(x, y, c) for y in range(SIDE)] for x in range(SIDE) for c in range(2)]
 SWAP = [(device(x, y, c), device(x, y, 1 - c)) for x in range(SIDE) for y in range(SIDE) for c in range(2)]
+
+
+def shift(dx, dy):
+    return [
+        (device(x, y, c), device((x + dx) % SIDE, (y + dy) % SIDE, c))
+        for x in range(SIDE)
+        for y in range(SIDE)
+        for c in range(2)
+    ]
 
 
 def shards(a_pieces, touched, slot_row, x_blocks, z_inverse, block_class):
     blocks = x_blocks.shape[0]
-    packed = call(
-        pack_kernel,
-        near_by(SIDE, DEPTH, WIDTH, dtype=BF16),
-        7,
-        2,
+    a_local = a_pieces[0]
+    slots = slot_row[None, :]
+    me = lax.axis_index("row").astype(jnp.int32).reshape(1)
+    classes = call(pack_kernel, near_by(SIDE, 16, WIDTH, dtype=BF16), 4, 1, grant=WIDE)(me, a_local, slots, touched)
+    mine = lax.all_to_all(classes, "row", 0, 0, tiled=True, axis_index_groups=LINES_X).reshape(ROWS, WIDTH)
+    own = call(
+        product_kernel,
+        near_by(SIDE, ROWS, WIDTH, dtype=BF16),
+        8,
+        3,
         (
             pltpu.VMEM((ROWS * 32, 128), F32),
             pltpu.VMEM((ROWS * 32, 128), F32),
@@ -313,20 +334,18 @@
             pltpu.VMEM((blocks, 2 * NB, 2 * NB), BF16),
             pltpu.VMEM((blocks, NB, 2 * NB), BF16),
         ),
-    )(touched, block_class, a_pieces[0], x_blocks, z_inverse, slot_row[None, :], touched)
-    lined = lax.all_to_all(packed, "row", 0, 0, tiled=True, axis_index_groups=LINES_X)
-    mine = lined[:, :16, :].reshape(ROWS, WIDTH)
-    near = lax.all_to_all(
-        jnp.broadcast_to(mine[None], (SIDE, ROWS, WIDTH)), "row", 0, 0, tiled=True, axis_index_groups=LINES_Y
-    )
+        grant=WIDE,
+    )(me, touched, block_class, a_local, x_blocks, z_inverse, slots, touched)
+    mine, own = lax.optimization_barrier((mine, own))
+    lined = lax.all_to_all(own, "row", 0, 0, tiled=True, axis_index_groups=LINES_X)
+    parts = [mine]
+    for n in (1, 3, 2):
+        parts.append(lax.ppermute(mine, "row", shift(0, n)))
+    near = jnp.stack(parts)
     far = lax.ppermute(near, "row", SWAP)
-    near_scores, col_ids, row_ids, rows = call(
-        near_kernel, (shape(256, 256), shape(256, 128, dtype=BF16), shape(256, 128, dtype=BF16), shape(8, 256)), 2
-    )(lined, near)
-    core = (lax.axis_index("row").astype(jnp.int32) & 1).reshape(1)
-    scores, cols = call(score_kernel, (near_by(16, SLAB, 128), near_by(8, 512)), 6, 1, held=())(
-        core, lined, far, near_scores, col_ids, row_ids
-    )
+    scores, cols, rows = call(
+        score_kernel, (near_by(16, SLAB, 128), near_by(8, 512), near_by(8, 256)), 3, held=(0, 1, 2)
+    )(lined, near, far)
     group = lax.axis_index("grp").astype(jnp.int32).reshape(1)
     sent, cols, rows, group = lax.optimization_barrier((scores.astype(jnp.float16), cols, rows, group))
     arrived = lax.all_to_all(sent, "grp", 0, 0, tiled=True).astype(F32)

time: 108 us -> 107 us (level)
  blocking collectives: 86.3 us -> 44.7 us
  waiting for transfers between devices: 0.01 us -> 25.5 us
  starting transfers between devices: 4.84 us -> 23.2 us
  Pallas kernels: 15.7 us -> 12.6 us
    all_to_all x2 -> x0, blocking collectives: 40.4 us -> none  [the longest x1 21.8 us: shards(): lax.all_to_all(jnp.broadcast_to(mine[None], (SIDE, ROWS, WIDTH)), 'row',...]
    all_to_all x0 -> x2, waiting for transfers between devices: none -> 15.6 us  [the longest x1 15.6 us: shards(): lax.all_to_all(own, 'row', 0, 0, tiled=True, axis_index_groups=LINES_X)]
    ppermute x0 -> x3, starting transfers between devices: none -> 10.1 us  [shards(): parts.append(lax.ppermute(mine, 'row', shift(0, n)))]
    ppermute x0 -> x3, waiting for transfers between devices: none -> 9.94 us  [shards(): parts.append(lax.ppermute(mine, 'row', shift(0, n)))]
    all_to_all x0 -> x2, starting transfers between devices: none -> 9.13 us  [the longest x1 4.83 us: shards(): lax.all_to_all(classes, 'row', 0, 0, tiled=True, axis_index_groups=LINES_X)]
    all_to_all x1, blocking collectives: 29.2 us -> 25.8 us  [shards(): arrived = lax.all_to_all(sent, 'grp', 0, 0, tiled=True).astype(F32)]
    pallas_call x5, Pallas kernels: 15.7 us -> 12.6 us  [placed(): run(*(pltpu.with_memory_space_constraint(a, pltpu.VMEM) if i in held else...]
    all_to_all x1, blocking collectives: 16.7 us -> 18.9 us  [shards(): lax.all_to_all(outgoing.reshape(32, 8, 128), 'row', 0, 0, tiled=True)]
  transfers between devices with their start and end apart: 1 -> 6, of which waited for: 0 -> 3; matrix products, arithmetic and copies ran while one was open for 0% -> 0% of each run, Pallas kernels for 3% -> 6%
where the time goes in v3:
time: 107 us; the launch traced here: 106 us
  blocking collectives  44.7 us (42%)
  waiting for transfers between devices  25.5 us (24%)
  starting transfers between devices  23.2 us (22%)
  Pallas kernels  12.6 us (12%)
    all_to_all x1, blocking collectives, shards(): arrived = lax.all_to_all(sent, 'grp', 0, 0, tiled=True).astype(F32)  25.8 us
    all_to_all x1, blocking collectives, shards(): lax.all_to_all(outgoing.reshape(32, 8, 128), 'row', 0, 0, tiled=True)  18.9 us
    all_to_all x1, waiting for transfers between devices, shards(): lax.all_to_all(own, 'row', 0, 0, tiled=True, axis_index_groups=LINES_X)  15.6 us
    pallas_call x5, Pallas kernels, placed(): run(*(pltpu.with_memory_space_constraint(a, pltpu.VMEM) if i in held else...  12.6 us
    ppermute x3, starting transfers between devices, shards(): parts.append(lax.ppermute(mine, 'row', shift(0, n)))  10.1 us
    ppermute x3, waiting for transfers between devices, shards(): parts.append(lax.ppermute(mine, 'row', shift(0, n)))  9.94 us
    all_to_all x1, starting transfers between devices, shards(): lax.all_to_all(classes, 'row', 0, 0, tiled=True, axis_index_groups=LINES_X)  4.83 us
    all_to_all x1, starting transfers between devices, shards(): lax.all_to_all(own, 'row', 0, 0, tiled=True, axis_index_groups=LINES_X)  4.3 us
  transfers between devices with their start and end apart: 6, of which 3 were waited for; matrix products, arithmetic and copies ran while one was open for 0% of the time, Pallas kernels for 6%

profile of v3, /device:TPU:1, one launch (start us, length us, event | category | flops | bytes accessed | tf_op | source)
XLA Modules:
  0.0 106.4 jit_solution(14757100671778334760)
XLA Ops:
  0.0 2.2 %shard_map.64 = bf16[4,16,2176]{2,1,0:T(8,128)(2,1)} custom-call(s32[1]{0:T(128)} %bitcast.me_ref, bf16[64,4096]{1,0:T(8,128)(2,1)} %bitcast.14, s32[1,64]{1,0:T(1,128)} %bitcast.24, s32[1,64]{1,0:T(1,128)} %touched_ref.3), custom_call_target="tpu_custom_call" | custom-call | tf_op jit(solution)/shard_map/pallas_call | solution.py:294
  2.2 4.8 %all-to-all-start = ((bf16[4,16,2176]{2,1,0:T(8,128)(2,1)}), bf16[4,16,2176]{2,1,0:T(8,128)(2,1)S(1)}, u32[]{:S(2)}, u32[]{:S(2)}) async-start(bf16[4,16,2176]{2,1,0:T(8,128)(2,1)} %shard_map.64), calls=%async_computation | async-start | bytes 557056 | tf_op jit(solution)/shard_map/all_to_all | solution.py:324
  7.0 6.6 %shard_map.65 = bf16[4,64,2176]{2,1,0:T(8,128)(2,1)} custom-call(s32[1]{0:T(128)} %bitcast.me_ref, s32[1,64]{1,0:T(1,128)} %touched_ref.3, s32[8]{0:T(128)} %class_ref.1, bf16[64,4096]{1,0:T(8,128)(2,1)} %bitcast.15, bf16[8,64,64]{2,1,0:T(8,128)(2,1)} %x_ref.1, bf16[8,64,64]{2,1,0:T(8,128)(2,1)} %z_ref.1, s32[1,64]{1,0:T(1,128)} %bitcast.25, s32[1,64]{1,0:T(1,128)} %touched_ref.3), custom_call_target="tpu_custom_call" | custom-call | tf_op jit(solution)/shard_map/pallas_call | solution.py:294
  13.6 0.0 all-to-all-done
  13.6 4.8 %collective-permute-start.2 = (bf16[64,2176]{1,0:T(8,128)(2,1)S(1)}, bf16[64,2176]{1,0:T(8,128)(2,1)S(1)}, u32[]{:S(2)}, u32[]{:S(2)}) collective-permute-start(bf16[64,2176]{1,0:T(8,128)(2,1)S(1)} %bitcast.16), channel_id=1, source_target_pairs={{0,4},{1,5},{2,6},{3,7},{4,0},{5,1},{6,2},{7,3},{8,12},{9,13},{10,... | collective-permute-start | bytes 835592 | tf_op jit(solution)/shard_map/ppermute | solution.py:343
  18.4 2.7 %collective-permute-start.1 = (bf16[64,2176]{1,0:T(8,128)(2,1)S(1)}, bf16[64,2176]{1,0:T(8,128)(2,1)S(1)}, u32[]{:S(2)}, u32[]{:S(2)}) collective-permute-start(bf16[64,2176]{1,0:T(8,128)(2,1)S(1)} %bitcast.17), channel_id=1, source_target_pairs={{0,6},{1,7},{2,0},{3,1},{4,2},{5,3},{6,4},{7,5},{8,14},{9,15},{10,... | collective-permute-start | bytes 835592 | tf_op jit(solution)/shard_map/ppermute | solution.py:343
  21.1 2.6 %collective-permute-start = (bf16[64,2176]{1,0:T(8,128)(2,1)S(1)}, bf16[64,2176]{1,0:T(8,128)(2,1)S(1)}, u32[]{:S(2)}, u32[]{:S(2)}) collective-permute-start(bf16[64,2176]{1,0:T(8,128)(2,1)S(1)} %bitcast.18), channel_id=1, source_target_pairs={{0,2},{1,3},{2,4},{3,5},{4,6},{5,7},{6,0},{7,1},{8,10},{9,11},{10,... | collective-permute-start | bytes 835592 | tf_op jit(solution)/shard_map/ppermute | solution.py:343
  23.7 0.0 collective-permute-done.2
  23.7 7.0 %collective-permute-done.1 = bf16[64,2176]{1,0:T(8,128)(2,1)S(1)} collective-permute-done((bf16[64,2176]{1,0:T(8,128)(2,1)S(1)}, bf16[64,2176]{1,0:T(8,128)(2,1)S(1)}, u32[]{:S(2)}, u32[]{:S(2)}) %collective-permute-start.1) | collective-permute-done | bytes 278560 | tf_op jit(solution)/shard_map/ppermute | solution.py:343
  30.7 2.9 %collective-permute-done = bf16[64,2176]{1,0:T(8,128)(2,1)S(1)} collective-permute-done((bf16[64,2176]{1,0:T(8,128)(2,1)S(1)}, bf16[64,2176]{1,0:T(8,128)(2,1)S(1)}, u32[]{:S(2)}, u32[]{:S(2)}) %collective-permute-start) | collective-permute-done | bytes 278560 | tf_op jit(solution)/shard_map/ppermute | solution.py:343
  33.7 0.2 pad_maximum_fusion.near_ref
  33.8 3.9 %collective-permute-start.3 = (bf16[4,64,2176]{2,1,0:T(8,128)(2,1)S(1)}, bf16[4,64,2176]{2,1,0:T(8,128)(2,1)S(1)}, u32[]{:S(2)}, u32[]{:S(2)}) collective-permute-start(bf16[4,64,2176]{2,1,0:T(8,128)(2,1)S(1)} %pad_maximum_fusion.near_ref), channel_id=1, source_target_pairs={{0,1},{1,0},{2,3},{3,2},{4,5},{5,4},{6,7},{7,6},{8,9},{9,8},{10,11... | collective-permute-start | bytes 3342344 | tf_op jit(solution)/shard_map/ppermute | solution.py:345
  37.8 4.3 %all-to-all-start.1 = ((bf16[4,64,2176]{2,1,0:T(8,128)(2,1)}), bf16[4,64,2176]{2,1,0:T(8,128)(2,1)S(1)}, u32[]{:S(2)}, u32[]{:S(2)}) async-start(bf16[4,64,2176]{2,1,0:T(8,128)(2,1)} %shard_map.65), calls=%async_computation.1 | async-start | bytes 2228224 | tf_op jit(solution)/shard_map/all_to_all | solution.py:340
  42.1 15.6 %all-to-all-done.1.rows_ref = bf16[4,64,2176]{2,1,0:T(8,128)(2,1)S(1)} async-done(((bf16[4,64,2176]{2,1,0:T(8,128)(2,1)}), bf16[4,64,2176]{2,1,0:T(8,128)(2,1)S(1)}, u32[]{:S(2)}, u32[]{:S(2)}) %all-to-all-start.1) | async-done | bytes 1114144 | tf_op jit(solution)/shard_map/all_to_all | solution.py:340
  57.7 0.0 collective-permute-done.3.far_ref
  57.7 1.9 %shard_map.66 = (f32[16,72,128]{2,1,0:T(8,128)S(1)}, f32[8,512]{1,0:T(8,128)S(1)}, f32[8,256]{1,0:T(8,128)S(1)}) custom-call(bf16[4,64,2176]{2,1,0:T(8,128)(2,1)S(1)} %all-to-all-done.1.rows_ref, bf16[4,64,2176]{2,1,0:T(8,128)(2,1)S(1)} %pad_maximum_fusion.near_ref, bf16[4,64,2176]{2,1,0:T(8,128)(2,1)S(1)} %collective-permute-done.3.far_ref), custom_call_target="tpu_custom_call" | custom-call | tf_op jit(solution)/shard_map/pallas_call | solution.py:294
  59.6 25.8 %all_to_all.20 = f16[16,72,128]{2,1,0:T(8,128)(2,1)S(1)} all-to-all(f16[16,72,128]{2,1,0:T(8,128)(2,1)S(1)} %convert_element_type.6), channel_id=1, replica_groups=mesh['grp'=16,'row'=32] {'grp'}, dimensions={0} | all-to-all | bytes 589824 | tf_op jit(solution)/shard_map/all_to_all | solution.py:351
  85.5 0.7 shard_map.67
  86.2 18.9 %all_to_all.21 = f32[32,8,128]{2,1,0:T(8,128)S(1)} all-to-all(f32[32,8,128]{2,1,0:T(8,128)S(1)} %bitcast.13), channel_id=1, replica_groups=mesh['grp'=16,'row'=32] {'row'}, dimensions={0} | all-to-all | bytes 262144 | tf_op jit(solution)/shard_map/all_to_all | solution.py:354
  105.1 1.4 %shard_map.68 = f32[64,128]{1,0:T(8,128)} custom-call(f32[256,128]{1,0:T(8,128)S(1)} %bitcast.12), custom_call_target="tpu_custom_call" | custom-call | tf_op jit(solution)/shard_map/pallas_call | solution.py:294
  (4 shorter events, 0.1 us)
Async XLA Ops:
  2.2 11.4 %all-to-all-start = ((bf16[4,16,2176]{2,1,0:T(8,128)(2,1)}), bf16[4,16,2176]{2,1,0:T(8,128)(2,1)S(1)}, u32[]{:S(2)}, u32[]{:S(2)}) async-start(bf16[4,16,2176]{2,1,0:T(8,128)(2,1)} %shard_map.64), calls=%async_computation | async-start | bytes 557056 | tf_op jit(solution)/shard_map/all_to_all | solution.py:324
  13.6 10.1 %collective-permute-start.2 = (bf16[64,2176]{1,0:T(8,128)(2,1)S(1)}, bf16[64,2176]{1,0:T(8,128)(2,1)S(1)}, u32[]{:S(2)}, u32[]{:S(2)}) collective-permute-start(bf16[64,2176]{1,0:T(8,128)(2,1)S(1)} %bitcast.16), channel_id=1, source_target_pairs={{0,4},{1,5},{2,6},{3,7},{4,0},{5,1},{6,2},{7,3},{8,12},{9,13},{10,... | collective-permute-start | bytes 835592 | tf_op jit(solution)/shard_map/ppermute | solution.py:343
  18.4 12.3 %collective-permute-start.1 = (bf16[64,2176]{1,0:T(8,128)(2,1)S(1)}, bf16[64,2176]{1,0:T(8,128)(2,1)S(1)}, u32[]{:S(2)}, u32[]{:S(2)}) collective-permute-start(bf16[64,2176]{1,0:T(8,128)(2,1)S(1)} %bitcast.17), channel_id=1, source_target_pairs={{0,6},{1,7},{2,0},{3,1},{4,2},{5,3},{6,4},{7,5},{8,14},{9,15},{10,... | collective-permute-start | bytes 835592 | tf_op jit(solution)/shard_map/ppermute | solution.py:343
  21.1 12.6 %collective-permute-start = (bf16[64,2176]{1,0:T(8,128)(2,1)S(1)}, bf16[64,2176]{1,0:T(8,128)(2,1)S(1)}, u32[]{:S(2)}, u32[]{:S(2)}) collective-permute-start(bf16[64,2176]{1,0:T(8,128)(2,1)S(1)} %bitcast.18), channel_id=1, source_target_pairs={{0,2},{1,3},{2,4},{3,5},{4,6},{5,7},{6,0},{7,1},{8,10},{9,11},{10,... | collective-permute-start | bytes 835592 | tf_op jit(solution)/shard_map/ppermute | solution.py:343
  33.8 23.8 %collective-permute-start.3 = (bf16[4,64,2176]{2,1,0:T(8,128)(2,1)S(1)}, bf16[4,64,2176]{2,1,0:T(8,128)(2,1)S(1)}, u32[]{:S(2)}, u32[]{:S(2)}) collective-permute-start(bf16[4,64,2176]{2,1,0:T(8,128)(2,1)S(1)} %pad_maximum_fusion.near_ref), channel_id=1, source_target_pairs={{0,1},{1,0},{2,3},{3,2},{4,5},{5,4},{6,7},{7,6},{8,9},{9,8},{10,11... | collective-permute-start | bytes 3342344 | tf_op jit(solution)/shard_map/ppermute | solution.py:345
  37.8 19.9 %all-to-all-start.1 = ((bf16[4,64,2176]{2,1,0:T(8,128)(2,1)}), bf16[4,64,2176]{2,1,0:T(8,128)(2,1)S(1)}, u32[]{:S(2)}, u32[]{:S(2)}) async-start(bf16[4,64,2176]{2,1,0:T(8,128)(2,1)} %shard_map.65), calls=%async_computation.1 | async-start | bytes 2228224 | tf_op jit(solution)/shard_map/all_to_all | solution.py:340

commit v4 on v3

--- a/solution.py
+++ b/solution.py
@@ -164,8 +164,8 @@
     chunks.append(with_ids(spill, columns, 0))
     for q, chunk in enumerate(chunks):
         picked = nn(select, chunk.astype(BF16)).astype(BF16)
-        for k in range(SIDE):
-            out_ref[k, :, q * 128 : (q + 1) * 128] = picked[16 * k : 16 * (k + 1)]
+        for k in range(SIDE * SIDE):
+            out_ref[k, :, q * 128 : (q + 1) * 128] = picked[16 * (k // SIDE) : 16 * (k // SIDE + 1)]
 
 
 def product_kernel(
@@ -178,14 +178,13 @@
     chunks, spill = folded(lambda q: both_ref[pl.ds(q, ROWS, stride=32), :], True)
     chunks.append(with_ids(spill, columns, 4))
     for q, chunk in enumerate(chunks):
-        rounded = chunk.astype(BF16)
-        for k in range(SIDE):
-            out_ref[k, :, q * 128 : (q + 1) * 128] = rounded
-
-
-def score_kernel(rows_ref, near_ref, far_ref, out_ref, col_ref, row_ref):
+        out_ref[:, q * 128 : (q + 1) * 128] = chunk.astype(BF16)
+
+
+def score_kernel(near_ref, far_ref, *refs):
+    row_refs, (out_ref, col_ref, row_ref) = refs[:SIDE], refs[SIDE:]
     n_rows, n_cols = 256, 512
-    rows = rows_ref[...].reshape(n_rows, WIDTH)
+    rows = jnp.concatenate([ref[...] for ref in row_refs], axis=0)
     near = near_ref[...].reshape(256, WIDTH)
     far = far_ref[...].reshape(256, WIDTH)
     scores = jnp.concatenate([nt(near, rows), nt(far, rows)], axis=0)
@@ -302,7 +301,7 @@
     return (x * SIDE + y) * 2 + c
 
 
-LINES_X = [[device(x, y, c) for x in range(SIDE)] for y in range(SIDE) for c in range(2)]
+PLANES = [[device(x, y, c) for x in range(SIDE) for y in range(SIDE)] for c in range(2)]
 SWAP = [(device(x, y, c), device(x, y, 1 - c)) for x in range(SIDE) for y in range(SIDE) for c in range(2)]
 
 
@@ -320,11 +319,13 @@
     a_local = a_pieces[0]
     slots = slot_row[None, :]
     me = lax.axis_index("row").astype(jnp.int32).reshape(1)
-    classes = call(pack_kernel, near_by(SIDE, 16, WIDTH, dtype=BF16), 4, 1, grant=WIDE)(me, a_local, slots, touched)
-    mine = lax.all_to_all(classes, "row", 0, 0, tiled=True, axis_index_groups=LINES_X).reshape(ROWS, WIDTH)
+    classes = call(pack_kernel, near_by(SIDE * SIDE, 16, WIDTH, dtype=BF16), 4, 1, grant=WIDE)(
+        me, a_local, slots, touched
+    )
+    near = lax.all_to_all(classes, "row", 0, 0, tiled=True, axis_index_groups=PLANES)
     own = call(
         product_kernel,
-        near_by(SIDE, ROWS, WIDTH, dtype=BF16),
+        near_by(ROWS, WIDTH, dtype=BF16),
         8,
         3,
         (
@@ -336,16 +337,13 @@
         ),
         grant=WIDE,
     )(me, touched, block_class, a_local, x_blocks, z_inverse, slots, touched)
-    mine, own = lax.optimization_barrier((mine, own))
-    lined = lax.all_to_all(own, "row", 0, 0, tiled=True, axis_index_groups=LINES_X)
-    parts = [mine]
-    for n in (1, 3, 2):
-        parts.append(lax.ppermute(mine, "row", shift(0, n)))
-    near = jnp.stack(parts)
+    lined = [own]
+    for n in (2, 1, 3):
+        lined.append(lax.ppermute(own, "row", shift(n, 0)))
     far = lax.ppermute(near, "row", SWAP)
     scores, cols, rows = call(
-        score_kernel, (near_by(16, SLAB, 128), near_by(8, 512), near_by(8, 256)), 3, held=(0, 1, 2)
-    )(lined, near, far)
+        score_kernel, (near_by(16, SLAB, 128), near_by(8, 512), near_by(8, 256)), 2 + SIDE, held=tuple(range(2 + SIDE))
+    )(near, far, *lined)
     group = lax.axis_index("grp").astype(jnp.int32).reshape(1)
     sent, cols, rows, group = lax.optimization_barrier((scores.astype(jnp.float16), cols, rows, group))
     arrived = lax.all_to_all(sent, "grp", 0, 0, tiled=True).astype(F32)

time: 107 us -> 106 us (level)
  blocking collectives: 44.7 us -> 69.7 us
  waiting for transfers between devices: 25.5 us -> 11.6 us
  starting transfers between devices: 23.2 us -> 13.1 us
  Pallas kernels: 12.6 us -> 10.9 us
    all_to_all x0 -> x1, blocking collectives: none -> 23.1 us  [shards(): lax.all_to_all(classes, 'row', 0, 0, tiled=True, axis_index_groups=PLANES)]
    all_to_all x2 -> x0, waiting for transfers between devices: 15.6 us -> none  [the longest x1 15.6 us: shards(): lax.all_to_all(own, 'row', 0, 0, tiled=True, axis_index_groups=LINES_X)]
    all_to_all x2 -> x0, starting transfers between devices: 9.13 us -> none  [the longest x1 4.83 us: shards(): lax.all_to_all(classes, 'row', 0, 0, tiled=True, axis_index_groups=LINES_X)]
    all_to_all x1, blocking collectives: 25.8 us -> 28.3 us  [shards(): arrived = lax.all_to_all(sent, 'grp', 0, 0, tiled=True).astype(F32)]
    ppermute x3, starting transfers between devices: 10.1 us -> 8.13 us  [shards(): lined.append(lax.ppermute(own, 'row', shift(n, 0)))]
    pallas_call x5, Pallas kernels: 12.6 us -> 10.9 us  [placed(): run(*(pltpu.with_memory_space_constraint(a, pltpu.VMEM) if i in held else...]
    ppermute x3, waiting for transfers between devices: 9.94 us -> 11.6 us  [shards(): lined.append(lax.ppermute(own, 'row', shift(n, 0)))]
    ppermute x1, starting transfers between devices: 3.93 us -> 5 us  [shards(): far = lax.ppermute(near, 'row', SWAP)]
  transfers between devices with their start and end apart: 6 -> 4, of which waited for: 3 -> 2; matrix products, arithmetic and copies ran while one was open for 0% -> 0% of each run, Pallas kernels for 6% -> 5%
where the time goes in v4:
time: 106 us
  blocking collectives  69.7 us (66%)
  starting transfers between devices  13.1 us (12%)
  waiting for transfers between devices  11.6 us (11%)
  Pallas kernels  10.9 us (10%)
    all_to_all x1, blocking collectives, shards(): arrived = lax.all_to_all(sent, 'grp', 0, 0, tiled=True).astype(F32)  28.3 us
    all_to_all x1, blocking collectives, shards(): lax.all_to_all(classes, 'row', 0, 0, tiled=True, axis_index_groups=PLANES)  23.1 us
    all_to_all x1, blocking collectives, shards(): lax.all_to_all(outgoing.reshape(32, 8, 128), 'row', 0, 0, tiled=True)  18.3 us
    ppermute x3, waiting for transfers between devices, shards(): lined.append(lax.ppermute(own, 'row', shift(n, 0)))  11.6 us
    pallas_call x5, Pallas kernels, placed(): run(*(pltpu.with_memory_space_constraint(a, pltpu.VMEM) if i in held else...  10.9 us
    ppermute x3, starting transfers between devices, shards(): lined.append(lax.ppermute(own, 'row', shift(n, 0)))  8.13 us
    ppermute x1, starting transfers between devices, shards(): far = lax.ppermute(near, 'row', SWAP)  5 us
  transfers between devices with their start and end apart: 4, of which 2 were waited for; matrix products, arithmetic and copies ran while one was open for 0% of the time, Pallas kernels for 5%

profile of v4, /device:TPU:1, one launch (start us, length us, event | category | flops | bytes accessed | tf_op | source)
XLA Modules:
  0.0 105.6 jit_solution(7478812843866738806)
XLA Ops:
  0.0 1.5 %shard_map.64 = bf16[16,16,2176]{2,1,0:T(8,128)(2,1)S(1)} custom-call(s32[1]{0:T(128)} %bitcast.me_ref, bf16[64,4096]{1,0:T(8,128)(2,1)} %bitcast.9, s32[1,64]{1,0:T(1,128)} %bitcast.12, s32[1,64]{1,0:T(1,128)} %touched_ref.3), custom_call_target="tpu_custom_call" | custom-call | tf_op jit(solution)/shard_map/pallas_call | solution.py:293
  1.5 23.1 %all_to_all.15.near_ref = bf16[16,16,2176]{2,1,0:T(8,128)(2,1)S(1)} all-to-all(bf16[16,16,2176]{2,1,0:T(8,128)(2,1)S(1)} %shard_map.64), channel_id=1, replica_groups={{0,2,4,6,8,10,12,14,16,18,20,22,24,26,28,30},{1,3,5,7,9,11,13,15,17,19,..., dimensions={0} | all-to-all | bytes 2228224 | tf_op jit(solution)/shard_map/all_to_all | solution.py:325
  24.5 5.0 %collective-permute-start = (bf16[16,16,2176]{2,1,0:T(8,128)(2,1)S(1)}, bf16[16,16,2176]{2,1,0:T(8,128)(2,1)S(1)}, u32[]{:S(2)}, u32[]{:S(2)}) collective-permute-start(bf16[16,16,2176]{2,1,0:T(8,128)(2,1)S(1)} %all_to_all.15.near_ref), channel_id=1, source_target_pairs={{0,1},{1,0},{2,3},{3,2},{4,5},{5,4},{6,7},{7,6},{8,9},{9,8},{10,11... | collective-permute-start | bytes 3342344 | tf_op jit(solution)/shard_map/ppermute | solution.py:343
  29.5 5.5 %shard_map.65.refs_0_ = bf16[64,2176]{1,0:T(8,128)(2,1)S(1)} custom-call(s32[1]{0:T(128)} %bitcast.me_ref, s32[1,64]{1,0:T(1,128)} %touched_ref.3, s32[8]{0:T(128)} %class_ref.1, bf16[64,4096]{1,0:T(8,128)(2,1)} %bitcast.10, bf16[8,64,64]{2,1,0:T(8,128)(2,1)} %x_ref.1, bf16[8,64,64]{2,1,0:T(8,128)(2,1)} %z_ref.1, s32[1,64]{1,0:T(1,128)} %bitcast.13, ...), custom_call_target="tpu_custom_call" | custom-call | tf_op jit(solution)/shard_map/pallas_call | solution.py:293
  35.1 2.8 %collective-permute-start.3 = (bf16[64,2176]{1,0:T(8,128)(2,1)S(1)}, bf16[64,2176]{1,0:T(8,128)(2,1)S(1)}, u32[]{:S(2)}, u32[]{:S(2)}) collective-permute-start(bf16[64,2176]{1,0:T(8,128)(2,1)S(1)} %shard_map.65.refs_0_), channel_id=1, source_target_pairs={{0,24},{1,25},{2,26},{3,27},{4,28},{5,29},{6,30},{7,31},{8,0},{9,1... | collective-permute-start | bytes 835592 | tf_op jit(solution)/shard_map/ppermute | solution.py:342
  37.8 2.5 %collective-permute-start.2 = (bf16[64,2176]{1,0:T(8,128)(2,1)S(1)}, bf16[64,2176]{1,0:T(8,128)(2,1)S(1)}, u32[]{:S(2)}, u32[]{:S(2)}) collective-permute-start(bf16[64,2176]{1,0:T(8,128)(2,1)S(1)} %shard_map.65.refs_0_), channel_id=1, source_target_pairs={{0,8},{1,9},{2,10},{3,11},{4,12},{5,13},{6,14},{7,15},{8,16},{9,17... | collective-permute-start | bytes 835592 | tf_op jit(solution)/shard_map/ppermute | solution.py:342
  40.4 2.8 %collective-permute-start.1 = (bf16[64,2176]{1,0:T(8,128)(2,1)S(1)}, bf16[64,2176]{1,0:T(8,128)(2,1)S(1)}, u32[]{:S(2)}, u32[]{:S(2)}) collective-permute-start(bf16[64,2176]{1,0:T(8,128)(2,1)S(1)} %shard_map.65.refs_0_), channel_id=1, source_target_pairs={{0,16},{1,17},{2,18},{3,19},{4,20},{5,21},{6,22},{7,23},{8,24},{9,... | collective-permute-start | bytes 835592 | tf_op jit(solution)/shard_map/ppermute | solution.py:342
  43.2 1.9 %collective-permute-done.3.refs_3_ = bf16[64,2176]{1,0:T(8,128)(2,1)S(1)} collective-permute-done((bf16[64,2176]{1,0:T(8,128)(2,1)S(1)}, bf16[64,2176]{1,0:T(8,128)(2,1)S(1)}, u32[]{:S(2)}, u32[]{:S(2)}) %collective-permute-start.3) | collective-permute-done | bytes 278560 | tf_op jit(solution)/shard_map/ppermute | solution.py:342
  45.2 9.7 %collective-permute-done.2.refs_2_ = bf16[64,2176]{1,0:T(8,128)(2,1)S(1)} collective-permute-done((bf16[64,2176]{1,0:T(8,128)(2,1)S(1)}, bf16[64,2176]{1,0:T(8,128)(2,1)S(1)}, u32[]{:S(2)}, u32[]{:S(2)}) %collective-permute-start.2) | collective-permute-done | bytes 278560 | tf_op jit(solution)/shard_map/ppermute | solution.py:342
  54.8 0.0 collective-permute-done.1.refs_1_
  54.8 0.0 collective-permute-done.far_ref
  54.8 1.9 %shard_map.66 = (f32[16,72,128]{2,1,0:T(8,128)S(1)}, f32[8,512]{1,0:T(8,128)S(1)}, f32[8,256]{1,0:T(8,128)S(1)}) custom-call(bf16[16,16,2176]{2,1,0:T(8,128)(2,1)S(1)} %all_to_all.15.near_ref, bf16[16,16,2176]{2,1,0:T(8,128)(2,1)S(1)} %collective-permute-done.far_ref, bf16[64,2176]{1,0:T(8,128)(2,1)S(1)} %shard_map.65.refs_0_, ...), custom_call_target="tpu_custom_call" | custom-call | tf_op jit(solution)/shard_map/pallas_call | solution.py:293
  56.8 28.3 %all_to_all.16 = f16[16,72,128]{2,1,0:T(8,128)(2,1)S(1)} all-to-all(f16[16,72,128]{2,1,0:T(8,128)(2,1)S(1)} %convert_element_type.6), channel_id=1, replica_groups=mesh['grp'=16,'row'=32] {'grp'}, dimensions={0} | all-to-all | bytes 589824 | tf_op jit(solution)/shard_map/all_to_all | solution.py:349
  85.2 0.7 shard_map.67
  85.9 18.3 %all_to_all.17 = f32[32,8,128]{2,1,0:T(8,128)S(1)} all-to-all(f32[32,8,128]{2,1,0:T(8,128)S(1)} %bitcast.8), channel_id=1, replica_groups=mesh['grp'=16,'row'=32] {'row'}, dimensions={0} | all-to-all | bytes 262144 | tf_op jit(solution)/shard_map/all_to_all | solution.py:352
  104.2 1.4 %shard_map.68 = f32[64,128]{1,0:T(8,128)} custom-call(f32[256,128]{1,0:T(8,128)S(1)} %bitcast.7), custom_call_target="tpu_custom_call" | custom-call | tf_op jit(solution)/shard_map/pallas_call | solution.py:293
  (4 shorter events, 0.1 us)
Async XLA Ops:
  24.5 30.3 %collective-permute-start = (bf16[16,16,2176]{2,1,0:T(8,128)(2,1)S(1)}, bf16[16,16,2176]{2,1,0:T(8,128)(2,1)S(1)}, u32[]{:S(2)}, u32[]{:S(2)}) collective-permute-start(bf16[16,16,2176]{2,1,0:T(8,128)(2,1)S(1)} %all_to_all.15.near_ref), channel_id=1, source_target_pairs={{0,1},{1,0},{2,3},{3,2},{4,5},{5,4},{6,7},{7,6},{8,9},{9,8},{10,11... | collective-permute-start | bytes 3342344 | tf_op jit(solution)/shard_map/ppermute | solution.py:343
  35.1 10.1 %collective-permute-start.3 = (bf16[64,2176]{1,0:T(8,128)(2,1)S(1)}, bf16[64,2176]{1,0:T(8,128)(2,1)S(1)}, u32[]{:S(2)}, u32[]{:S(2)}) collective-permute-start(bf16[64,2176]{1,0:T(8,128)(2,1)S(1)} %shard_map.65.refs_0_), channel_id=1, source_target_pairs={{0,24},{1,25},{2,26},{3,27},{4,28},{5,29},{6,30},{7,31},{8,0},{9,1... | collective-permute-start | bytes 835592 | tf_op jit(solution)/shard_map/ppermute | solution.py:342
  37.8 17.0 %collective-permute-start.2 = (bf16[64,2176]{1,0:T(8,128)(2,1)S(1)}, bf16[64,2176]{1,0:T(8,128)(2,1)S(1)}, u32[]{:S(2)}, u32[]{:S(2)}) collective-permute-start(bf16[64,2176]{1,0:T(8,128)(2,1)S(1)} %shard_map.65.refs_0_), channel_id=1, source_target_pairs={{0,8},{1,9},{2,10},{3,11},{4,12},{5,13},{6,14},{7,15},{8,16},{9,17... | collective-permute-start | bytes 835592 | tf_op jit(solution)/shard_map/ppermute | solution.py:342
  40.4 14.5 %collective-permute-start.1 = (bf16[64,2176]{1,0:T(8,128)(2,1)S(1)}, bf16[64,2176]{1,0:T(8,128)(2,1)S(1)}, u32[]{:S(2)}, u32[]{:S(2)}) collective-permute-start(bf16[64,2176]{1,0:T(8,128)(2,1)S(1)} %shard_map.65.refs_0_), channel_id=1, source_target_pairs={{0,16},{1,17},{2,18},{3,19},{4,20},{5,21},{6,22},{7,23},{8,24},{9,... | collective-permute-start | bytes 835592 | tf_op jit(solution)/shard_map/ppermute | solution.py:342

commit v5 on v4

--- a/solution.py
+++ b/solution.py
@@ -13,7 +13,7 @@
 ROWS = 64
 SIDE = 4
 SLAB = 72
-QUADS = 8
+QUADS = 16
 GRANT = 16 << 20
 WIDE = 60 << 20
 VMEM = pl.BlockSpec(memory_space=pltpu.VMEM)
@@ -181,35 +181,43 @@
         out_ref[:, q * 128 : (q + 1) * 128] = chunk.astype(BF16)
 
 
-def score_kernel(near_ref, far_ref, *refs):
-    row_refs, (out_ref, col_ref, row_ref) = refs[:SIDE], refs[SIDE:]
-    n_rows, n_cols = 256, 512
+def order_kernel(near_ref, far_ref, move_ref, kind_ref, col_ref):
+    n_cols = 512
+    last = slice(16 * 128, WIDTH)
+    ids = [ref[:, :, last].reshape(256, 128) for ref in (near_ref, far_ref)]
+    col_ids = jnp.concatenate(ids, axis=0)
+    col_t = nt(ones_where(iota((8, 128), 0) == iota((8, 128), 1), BF16), col_ids)
+    col_f = col_ids.astype(F32)
+    own = ones_where(col_f[:, 1:2] == iota((n_cols, 128), 1).astype(F32), BF16)
+    rank = jnp.sum(jnp.where(col_f[:, 3:4] < col_t[3:4, :], nt(own, own), 0.0), axis=0, keepdims=True)
+    place = col_t[1:2, :] * 16.0 + rank
+    move = ones_where(iota((n_cols, n_cols), 0).astype(F32) == place, BF16)
+    move_ref[...] = move
+    kind_ref[...] = col_f
+    odd = col_t[1:2, :] - 2.0 * jnp.floor(col_t[1:2, :] * 0.5)
+    col_id = (odd * 64.0 + col_t[2:3, :]).astype(BF16)
+    col_ref[...] = nt(jnp.broadcast_to(col_id, (8, n_cols)), move)
+
+
+def score_kernel(near_ref, far_ref, move_ref, kind_ref, *refs):
+    row_refs, (out_ref, row_ref) = refs[:SIDE], refs[SIDE:]
+    n_rows = 256
     rows = jnp.concatenate([ref[...] for ref in row_refs], axis=0)
     near = near_ref[...].reshape(256, WIDTH)
     far = far_ref[...].reshape(256, WIDTH)
     scores = jnp.concatenate([nt(near, rows), nt(far, rows)], axis=0)
-    col_ids = jnp.concatenate([near[:, 16 * 128 :], far[:, 16 * 128 :]], axis=0)
     row_ids = rows[:, 16 * 128 :]
-    pick = iota((8, 128), 0)
-    spot = iota((8, 128), 1)
-    col_t = nt(ones_where(pick == spot, BF16), col_ids)
-    row_t = nt(ones_where(pick + 4 == spot, BF16), row_ids)
-    col_f = col_ids.astype(F32)
+    row_t = nt(ones_where(iota((8, 128), 0) + 4 == iota((8, 128), 1), BF16), row_ids)
     row_f = row_ids.astype(F32)
-    lane_r = iota((n_rows, 128), 1).astype(F32)
-    own_r = ones_where(row_f[:, 5:6] == lane_r, BF16)
+    own_r = ones_where(row_f[:, 5:6] == iota((n_rows, 128), 1).astype(F32), BF16)
     before = (iota((n_rows, n_rows), 0) < iota((n_rows, n_rows), 1)) & (row_f[:, 7:8] == row_t[3:4, :])
     row_rank = jnp.sum(jnp.where(before, nt(own_r, own_r), 0.0), axis=0, keepdims=True)
     row_ref[0:1, :] = row_t[1:2, :] * 8.0 + jnp.floor(row_t[3:4, :] * 0.125)
     row_ref[1:2, :] = row_rank
     row_ref[2:3, :] = row_t[2:3, :] + 1.0
     row_ref[3:8, :] = jnp.zeros((5, n_rows), F32)
-    scores = jnp.where(col_f[:, 0:1] == row_t[0:1, :], scores, 0.0)
-    lane_c = iota((n_cols, 128), 1).astype(F32)
-    own_c = ones_where(col_f[:, 1:2] == lane_c, BF16)
-    rank = jnp.sum(jnp.where(col_f[:, 3:4] < col_t[3:4, :], nt(own_c, own_c), 0.0), axis=0, keepdims=True)
-    place = col_t[1:2, :] * 16.0 + rank
-    move = ones_where(iota((n_cols, n_cols), 0).astype(F32) == place, BF16)
+    move = move_ref[...]
+    scores = jnp.where(kind_ref[:, 0:1] == row_t[0:1, :], scores, 0.0)
     top = jnp.max(jnp.max(jnp.abs(scores), axis=0, keepdims=True), axis=1, keepdims=True)
     power = jnp.ceil(jnp.log(jnp.maximum(top, 1e-36)) * 1.4426950408889634)
     scaled = scores * jnp.exp2(-power)
@@ -221,9 +229,6 @@
         out_ref[g, 0:32, :] = moved[32 * g : 32 * (g + 1), 0:128]
         out_ref[g, 32:64, :] = moved[32 * g : 32 * (g + 1), 128:256]
         out_ref[g, 64:72, :] = note
-    odd = col_t[1:2, :] - 2.0 * jnp.floor(col_t[1:2, :] * 0.5)
-    col_id = (odd * 64.0 + col_t[2:3, :]).astype(BF16)
-    col_ref[...] = nt(jnp.broadcast_to(col_id, (8, n_cols)), move)
 
 
 def send_kernel(group_ref, total_ref, col_ref, row_ref, out_ref):
@@ -256,13 +261,13 @@
     is_value = (iota((64, 64), 0) & 7) < 4
     spot = iota((64, 64), 1).astype(F32) + 1.0
     place = jnp.concatenate(
-        [ones_where(is_value & (high[:, 32 * k : 32 * k + 1] == spot), BF16) for k in range(SIDE)], axis=0
-    )
-    own = [jnp.where(lane == k, wide, 0.0) for k in range(SIDE)]
-    total = None
-    for part in thirds(jnp.concatenate(own, axis=0)):
+        [ones_where(is_value & (high[:, 32 * k : 32 * k + 1] == spot), BF16) for k in range(SIDE)], axis=1
+    )
+    found = None
+    for part in thirds(wide):
         term = tn(place, part)
-        total = term if total is None else total + term
+        found = term if found is None else found + term
+    total = jnp.where(lane == 0, found[0:64], jnp.where(lane == 1, found[64:128], jnp.where(lane == 2, found[128:192], found[192:256])))
     id_row = wide[4:5, :]
     col = id_row - 128.0 * jnp.floor(id_row * (1.0 / 128.0))
     spread = ones_where(iota((128, 512), 0).astype(F32) == col, BF16)
@@ -341,9 +346,12 @@
     for n in (2, 1, 3):
         lined.append(lax.ppermute(own, "row", shift(n, 0)))
     far = lax.ppermute(near, "row", SWAP)
-    scores, cols, rows = call(
-        score_kernel, (near_by(16, SLAB, 128), near_by(8, 512), near_by(8, 256)), 2 + SIDE, held=tuple(range(2 + SIDE))
-    )(near, far, *lined)
+    move, kinds, cols = call(
+        order_kernel, (near_by(512, 512, dtype=BF16), near_by(512, 128), near_by(8, 512)), 2, held=(0, 1)
+    )(near, far)
+    scores, rows = call(score_kernel, (near_by(16, SLAB, 128), near_by(8, 256)), 4 + SIDE, held=tuple(range(4 + SIDE)))(
+        near, far, move, kinds, *lined
+    )
     group = lax.axis_index("grp").astype(jnp.int32).reshape(1)
     sent, cols, rows, group = lax.optimization_barrier((scores.astype(jnp.float16), cols, rows, group))
     arrived = lax.all_to_all(sent, "grp", 0, 0, tiled=True).astype(F32)

time: 106 us -> 105 us (level)
    pallas_call x5 -> x6, Pallas kernels: 10.9 us -> 10.7 us  [placed(): run(*(pltpu.with_memory_space_constraint(a, pltpu.VMEM) if i in held else...]
where the time goes in v5:
time: 105 us
  blocking collectives  69.8 us (66%)
  starting transfers between devices  13.1 us (12%)
  waiting for transfers between devices  11 us (10%)
  Pallas kernels  10.7 us (10%)
    all_to_all x1, blocking collectives, shards(): arrived = lax.all_to_all(sent, 'grp', 0, 0, tiled=True).astype(F32)  28.3 us
    all_to_all x1, blocking collectives, shards(): lax.all_to_all(classes, 'row', 0, 0, tiled=True, axis_index_groups=PLANES)  23.1 us
    all_to_all x1, blocking collectives, shards(): lax.all_to_all(outgoing.reshape(32, 8, 128), 'row', 0, 0, tiled=True)  18.4 us
    ppermute x3, waiting for transfers between devices, shards(): lined.append(lax.ppermute(own, 'row', shift(n, 0)))  11 us
    pallas_call x6, Pallas kernels, placed(): run(*(pltpu.with_memory_space_constraint(a, pltpu.VMEM) if i in held else...  10.7 us
    ppermute x3, starting transfers between devices, shards(): lined.append(lax.ppermute(own, 'row', shift(n, 0)))  8.12 us
    ppermute x1, starting transfers between devices, shards(): far = lax.ppermute(near, 'row', SWAP)  5 us
  transfers between devices with their start and end apart: 4, of which 2 were waited for; matrix products, arithmetic and copies ran while one was open for 0% of the time, Pallas kernels for 5%

profile of v5, /device:TPU:1, one launch (start us, length us, event | category | flops | bytes accessed | tf_op | source)
XLA Modules:
  0.0 104.8 jit_solution(10941162330644508421)
XLA Ops:
  0.0 1.5 %shard_map.64 = bf16[16,16,2176]{2,1,0:T(8,128)(2,1)S(1)} custom-call(s32[1]{0:T(128)} %bitcast.me_ref, bf16[64,4096]{1,0:T(8,128)(2,1)} %bitcast.9, s32[1,64]{1,0:T(1,128)} %bitcast.12, s32[1,64]{1,0:T(1,128)} %touched_ref.3), custom_call_target="tpu_custom_call" | custom-call | tf_op jit(solution)/shard_map/pallas_call | solution.py:298
  1.5 23.1 %all_to_all.15.near_ref = bf16[16,16,2176]{2,1,0:T(8,128)(2,1)S(1)} all-to-all(bf16[16,16,2176]{2,1,0:T(8,128)(2,1)S(1)} %shard_map.64), channel_id=1, replica_groups={{0,2,4,6,8,10,12,14,16,18,20,22,24,26,28,30},{1,3,5,7,9,11,13,15,17,19,..., dimensions={0} | all-to-all | bytes 2228224 | tf_op jit(solution)/shard_map/all_to_all | solution.py:330
  24.5 5.0 %collective-permute-start = (bf16[16,16,2176]{2,1,0:T(8,128)(2,1)S(1)}, bf16[16,16,2176]{2,1,0:T(8,128)(2,1)S(1)}, u32[]{:S(2)}, u32[]{:S(2)}) collective-permute-start(bf16[16,16,2176]{2,1,0:T(8,128)(2,1)S(1)} %all_to_all.15.near_ref), channel_id=1, source_target_pairs={{0,1},{1,0},{2,3},{3,2},{4,5},{5,4},{6,7},{7,6},{8,9},{9,8},{10,11... | collective-permute-start | bytes 3342344 | tf_op jit(solution)/shard_map/ppermute | solution.py:348
  29.5 5.0 %shard_map.66.refs_0_ = bf16[64,2176]{1,0:T(8,128)(2,1)S(1)} custom-call(s32[1]{0:T(128)} %bitcast.me_ref, s32[1,64]{1,0:T(1,128)} %touched_ref.3, s32[8]{0:T(128)} %class_ref.1, bf16[64,4096]{1,0:T(8,128)(2,1)} %bitcast.10, bf16[8,64,64]{2,1,0:T(8,128)(2,1)} %x_ref.1, bf16[8,64,64]{2,1,0:T(8,128)(2,1)} %z_ref.1, s32[1,64]{1,0:T(1,128)} %bitcast.13, ...), custom_call_target="tpu_custom_call" | custom-call | tf_op jit(solution)/shard_map/pallas_call | solution.py:298
  34.5 2.7 %collective-permute-start.3 = (bf16[64,2176]{1,0:T(8,128)(2,1)S(1)}, bf16[64,2176]{1,0:T(8,128)(2,1)S(1)}, u32[]{:S(2)}, u32[]{:S(2)}) collective-permute-start(bf16[64,2176]{1,0:T(8,128)(2,1)S(1)} %shard_map.66.refs_0_), channel_id=1, source_target_pairs={{0,24},{1,25},{2,26},{3,27},{4,28},{5,29},{6,30},{7,31},{8,0},{9,1... | collective-permute-start | bytes 835592 | tf_op jit(solution)/shard_map/ppermute | solution.py:347
  37.3 2.5 %collective-permute-start.2 = (bf16[64,2176]{1,0:T(8,128)(2,1)S(1)}, bf16[64,2176]{1,0:T(8,128)(2,1)S(1)}, u32[]{:S(2)}, u32[]{:S(2)}) collective-permute-start(bf16[64,2176]{1,0:T(8,128)(2,1)S(1)} %shard_map.66.refs_0_), channel_id=1, source_target_pairs={{0,8},{1,9},{2,10},{3,11},{4,12},{5,13},{6,14},{7,15},{8,16},{9,17... | collective-permute-start | bytes 835592 | tf_op jit(solution)/shard_map/ppermute | solution.py:347
  39.8 2.8 %collective-permute-start.1 = (bf16[64,2176]{1,0:T(8,128)(2,1)S(1)}, bf16[64,2176]{1,0:T(8,128)(2,1)S(1)}, u32[]{:S(2)}, u32[]{:S(2)}) collective-permute-start(bf16[64,2176]{1,0:T(8,128)(2,1)S(1)} %shard_map.66.refs_0_), channel_id=1, source_target_pairs={{0,16},{1,17},{2,18},{3,19},{4,20},{5,21},{6,22},{7,23},{8,24},{9,... | collective-permute-start | bytes 835592 | tf_op jit(solution)/shard_map/ppermute | solution.py:347
  42.7 0.0 collective-permute-done.far_ref
  42.7 0.6 shard_map.65
  43.3 1.3 %collective-permute-done.3.refs_3_ = bf16[64,2176]{1,0:T(8,128)(2,1)S(1)} collective-permute-done((bf16[64,2176]{1,0:T(8,128)(2,1)S(1)}, bf16[64,2176]{1,0:T(8,128)(2,1)S(1)}, u32[]{:S(2)}, u32[]{:S(2)}) %collective-permute-start.3) | collective-permute-done | bytes 278560 | tf_op jit(solution)/shard_map/ppermute | solution.py:347
  44.6 9.6 %collective-permute-done.2.refs_2_ = bf16[64,2176]{1,0:T(8,128)(2,1)S(1)} collective-permute-done((bf16[64,2176]{1,0:T(8,128)(2,1)S(1)}, bf16[64,2176]{1,0:T(8,128)(2,1)S(1)}, u32[]{:S(2)}, u32[]{:S(2)}) %collective-permute-start.2) | collective-permute-done | bytes 278560 | tf_op jit(solution)/shard_map/ppermute | solution.py:347
  54.3 0.0 collective-permute-done.1.refs_1_
  54.3 1.5 %shard_map.67 = (f32[16,72,128]{2,1,0:T(8,128)S(1)}, f32[8,256]{1,0:T(8,128)S(1)}) custom-call(bf16[16,16,2176]{2,1,0:T(8,128)(2,1)S(1)} %all_to_all.15.near_ref, bf16[16,16,2176]{2,1,0:T(8,128)(2,1)S(1)} %collective-permute-done.far_ref, bf16[512,512]{1,0:T(8,128)(2,1)S(1)} %get-tuple-element.14.move_ref, f32[512,128]{1,0:T(8,128)S(1)} %get-tuple-element.15.kind_ref, ...), custom_call_target="tpu_custom_call" | custom-call | tf_op jit(solution)/shard_map/pallas_call | solution.py:298
  55.8 28.3 %all_to_all.16 = f16[16,72,128]{2,1,0:T(8,128)(2,1)S(1)} all-to-all(f16[16,72,128]{2,1,0:T(8,128)(2,1)S(1)} %convert_element_type.6), channel_id=1, replica_groups=mesh['grp'=16,'row'=32] {'grp'}, dimensions={0} | all-to-all | bytes 589824 | tf_op jit(solution)/shard_map/all_to_all | solution.py:357
  84.3 0.7 shard_map.68
  84.9 18.4 %all_to_all.17 = f32[32,8,128]{2,1,0:T(8,128)S(1)} all-to-all(f32[32,8,128]{2,1,0:T(8,128)S(1)} %bitcast.8), channel_id=1, replica_groups=mesh['grp'=16,'row'=32] {'row'}, dimensions={0} | all-to-all | bytes 262144 | tf_op jit(solution)/shard_map/all_to_all | solution.py:360
  103.3 1.5 %shard_map.69 = f32[64,128]{1,0:T(8,128)} custom-call(f32[256,128]{1,0:T(8,128)S(1)} %bitcast.7), custom_call_target="tpu_custom_call" | custom-call | tf_op jit(solution)/shard_map/pallas_call | solution.py:298
  (4 shorter events, 0.1 us)
Async XLA Ops:
  24.5 18.1 %collective-permute-start = (bf16[16,16,2176]{2,1,0:T(8,128)(2,1)S(1)}, bf16[16,16,2176]{2,1,0:T(8,128)(2,1)S(1)}, u32[]{:S(2)}, u32[]{:S(2)}) collective-permute-start(bf16[16,16,2176]{2,1,0:T(8,128)(2,1)S(1)} %all_to_all.15.near_ref), channel_id=1, source_target_pairs={{0,1},{1,0},{2,3},{3,2},{4,5},{5,4},{6,7},{7,6},{8,9},{9,8},{10,11... | collective-permute-start | bytes 3342344 | tf_op jit(solution)/shard_map/ppermute | solution.py:348
  34.5 10.1 %collective-permute-start.3 = (bf16[64,2176]{1,0:T(8,128)(2,1)S(1)}, bf16[64,2176]{1,0:T(8,128)(2,1)S(1)}, u32[]{:S(2)}, u32[]{:S(2)}) collective-permute-start(bf16[64,2176]{1,0:T(8,128)(2,1)S(1)} %shard_map.66.refs_0_), channel_id=1, source_target_pairs={{0,24},{1,25},{2,26},{3,27},{4,28},{5,29},{6,30},{7,31},{8,0},{9,1... | collective-permute-start | bytes 835592 | tf_op jit(solution)/shard_map/ppermute | solution.py:347
  37.3 17.0 %collective-permute-start.2 = (bf16[64,2176]{1,0:T(8,128)(2,1)S(1)}, bf16[64,2176]{1,0:T(8,128)(2,1)S(1)}, u32[]{:S(2)}, u32[]{:S(2)}) collective-permute-start(bf16[64,2176]{1,0:T(8,128)(2,1)S(1)} %shard_map.66.refs_0_), channel_id=1, source_target_pairs={{0,8},{1,9},{2,10},{3,11},{4,12},{5,13},{6,14},{7,15},{8,16},{9,17... | collective-permute-start | bytes 835592 | tf_op jit(solution)/shard_map/ppermute | solution.py:347
  39.8 14.5 %collective-permute-start.1 = (bf16[64,2176]{1,0:T(8,128)(2,1)S(1)}, bf16[64,2176]{1,0:T(8,128)(2,1)S(1)}, u32[]{:S(2)}, u32[]{:S(2)}) collective-permute-start(bf16[64,2176]{1,0:T(8,128)(2,1)S(1)} %shard_map.66.refs_0_), channel_id=1, source_target_pairs={{0,16},{1,17},{2,18},{3,19},{4,20},{5,21},{6,22},{7,23},{8,24},{9,... | collective-permute-start | bytes 835592 | tf_op jit(solution)/shard_map/ppermute | solution.py:347

commit v6 on v5

--- a/solution.py
+++ b/solution.py
@@ -78,7 +78,7 @@
         active = (NB // 2) * (1 + class_ref[k])
         inside = (rr < active) & (cc < active)
         x = jnp.where(inside, x_ref[k].astype(F32), 0.0).astype(BF16)
-        z = jnp.where(inside, z_ref[k].astype(F32), 0.0).astype(BF16)
+        z = jnp.where(inside, z_ref[k].astype(F32) * 0.5, 0.0).astype(BF16)
         half = nt(x, turn).astype(BF16)
         full = nn(turn, half).astype(BF16)
         left_ref[k, 0:NB, :] = beside(full, full)
@@ -219,12 +219,12 @@
     move = move_ref[...]
     scores = jnp.where(kind_ref[:, 0:1] == row_t[0:1, :], scores, 0.0)
     top = jnp.max(jnp.max(jnp.abs(scores), axis=0, keepdims=True), axis=1, keepdims=True)
-    power = jnp.ceil(jnp.log(jnp.maximum(top, 1e-36)) * 1.4426950408889634)
+    power = jnp.minimum(jnp.ceil(jnp.log(jnp.maximum(top, 1e-36)) * 1.4426950408889634), 126.0)
     scaled = scores * jnp.exp2(-power)
     high = scaled.astype(BF16)
     low = (scaled - high.astype(F32)).astype(BF16)
     moved = nn(move, high) + nn(move, low)
-    note = jnp.broadcast_to(power, (8, 128))
+    note = jnp.broadcast_to(power + 1.0, (8, 128))
     for g in range(16):
         out_ref[g, 0:32, :] = moved[32 * g : 32 * (g + 1), 0:128]
         out_ref[g, 32:64, :] = moved[32 * g : 32 * (g + 1), 128:256]

time: 105 us -> 105 us (level)
  no operation moved by 1% of the time
where the time goes in v6:
time: 105 us
  blocking collectives  69.8 us (66%)
  starting transfers between devices  13.1 us (12%)
  waiting for transfers between devices  11 us (10%)
  Pallas kernels  10.7 us (10%)
    all_to_all x1, blocking collectives, shards(): arrived = lax.all_to_all(sent, 'grp', 0, 0, tiled=True).astype(F32)  28.3 us
    all_to_all x1, blocking collectives, shards(): lax.all_to_all(classes, 'row', 0, 0, tiled=True, axis_index_groups=PLANES)  23.1 us
    all_to_all x1, blocking collectives, shards(): lax.all_to_all(outgoing.reshape(32, 8, 128), 'row', 0, 0, tiled=True)  18.4 us
    ppermute x3, waiting for transfers between devices, shards(): lined.append(lax.ppermute(own, 'row', shift(n, 0)))  11 us
    pallas_call x6, Pallas kernels, placed(): run(*(pltpu.with_memory_space_constraint(a, pltpu.VMEM) if i in held else...  10.7 us
    ppermute x3, starting transfers between devices, shards(): lined.append(lax.ppermute(own, 'row', shift(n, 0)))  8.13 us
    ppermute x1, starting transfers between devices, shards(): far = lax.ppermute(near, 'row', SWAP)  5 us
  transfers between devices with their start and end apart: 4, of which 2 were waited for; matrix products, arithmetic and copies ran while one was open for 0% of the time, Pallas kernels for 5%

profile of v6, /device:TPU:1, one launch (start us, length us, event | category | flops | bytes accessed | tf_op | source)
XLA Modules:
  0.0 104.8 jit_solution(5808748367110488588)
XLA Ops:
  0.0 1.5 %shard_map.64 = bf16[16,16,2176]{2,1,0:T(8,128)(2,1)S(1)} custom-call(s32[1]{0:T(128)} %bitcast.me_ref, bf16[64,4096]{1,0:T(8,128)(2,1)} %bitcast.9, s32[1,64]{1,0:T(1,128)} %bitcast.12, s32[1,64]{1,0:T(1,128)} %touched_ref.3), custom_call_target="tpu_custom_call" | custom-call | tf_op jit(solution)/shard_map/pallas_call | solution.py:298
  1.5 23.1 %all_to_all.15.near_ref = bf16[16,16,2176]{2,1,0:T(8,128)(2,1)S(1)} all-to-all(bf16[16,16,2176]{2,1,0:T(8,128)(2,1)S(1)} %shard_map.64), channel_id=1, replica_groups={{0,2,4,6,8,10,12,14,16,18,20,22,24,26,28,30},{1,3,5,7,9,11,13,15,17,19,..., dimensions={0} | all-to-all | bytes 2228224 | tf_op jit(solution)/shard_map/all_to_all | solution.py:330
  24.5 5.0 %collective-permute-start = (bf16[16,16,2176]{2,1,0:T(8,128)(2,1)S(1)}, bf16[16,16,2176]{2,1,0:T(8,128)(2,1)S(1)}, u32[]{:S(2)}, u32[]{:S(2)}) collective-permute-start(bf16[16,16,2176]{2,1,0:T(8,128)(2,1)S(1)} %all_to_all.15.near_ref), channel_id=1, source_target_pairs={{0,1},{1,0},{2,3},{3,2},{4,5},{5,4},{6,7},{7,6},{8,9},{9,8},{10,11... | collective-permute-start | bytes 3342344 | tf_op jit(solution)/shard_map/ppermute | solution.py:348
  29.5 5.0 %shard_map.66.refs_0_ = bf16[64,2176]{1,0:T(8,128)(2,1)S(1)} custom-call(s32[1]{0:T(128)} %bitcast.me_ref, s32[1,64]{1,0:T(1,128)} %touched_ref.3, s32[8]{0:T(128)} %class_ref.1, bf16[64,4096]{1,0:T(8,128)(2,1)} %bitcast.10, bf16[8,64,64]{2,1,0:T(8,128)(2,1)} %x_ref.1, bf16[8,64,64]{2,1,0:T(8,128)(2,1)} %z_ref.1, s32[1,64]{1,0:T(1,128)} %bitcast.13, ...), custom_call_target="tpu_custom_call" | custom-call | tf_op jit(solution)/shard_map/pallas_call | solution.py:298
  34.5 2.8 %collective-permute-start.3 = (bf16[64,2176]{1,0:T(8,128)(2,1)S(1)}, bf16[64,2176]{1,0:T(8,128)(2,1)S(1)}, u32[]{:S(2)}, u32[]{:S(2)}) collective-permute-start(bf16[64,2176]{1,0:T(8,128)(2,1)S(1)} %shard_map.66.refs_0_), channel_id=1, source_target_pairs={{0,24},{1,25},{2,26},{3,27},{4,28},{5,29},{6,30},{7,31},{8,0},{9,1... | collective-permute-start | bytes 835592 | tf_op jit(solution)/shard_map/ppermute | solution.py:347
  37.3 2.5 %collective-permute-start.2 = (bf16[64,2176]{1,0:T(8,128)(2,1)S(1)}, bf16[64,2176]{1,0:T(8,128)(2,1)S(1)}, u32[]{:S(2)}, u32[]{:S(2)}) collective-permute-start(bf16[64,2176]{1,0:T(8,128)(2,1)S(1)} %shard_map.66.refs_0_), channel_id=1, source_target_pairs={{0,8},{1,9},{2,10},{3,11},{4,12},{5,13},{6,14},{7,15},{8,16},{9,17... | collective-permute-start | bytes 835592 | tf_op jit(solution)/shard_map/ppermute | solution.py:347
  39.8 2.8 %collective-permute-start.1 = (bf16[64,2176]{1,0:T(8,128)(2,1)S(1)}, bf16[64,2176]{1,0:T(8,128)(2,1)S(1)}, u32[]{:S(2)}, u32[]{:S(2)}) collective-permute-start(bf16[64,2176]{1,0:T(8,128)(2,1)S(1)} %shard_map.66.refs_0_), channel_id=1, source_target_pairs={{0,16},{1,17},{2,18},{3,19},{4,20},{5,21},{6,22},{7,23},{8,24},{9,... | collective-permute-start | bytes 835592 | tf_op jit(solution)/shard_map/ppermute | solution.py:347
  42.7 0.0 collective-permute-done.far_ref
  42.7 0.6 shard_map.65
  43.3 1.3 %collective-permute-done.3.refs_3_ = bf16[64,2176]{1,0:T(8,128)(2,1)S(1)} collective-permute-done((bf16[64,2176]{1,0:T(8,128)(2,1)S(1)}, bf16[64,2176]{1,0:T(8,128)(2,1)S(1)}, u32[]{:S(2)}, u32[]{:S(2)}) %collective-permute-start.3) | collective-permute-done | bytes 278560 | tf_op jit(solution)/shard_map/ppermute | solution.py:347
  44.6 9.7 %collective-permute-done.2.refs_2_ = bf16[64,2176]{1,0:T(8,128)(2,1)S(1)} collective-permute-done((bf16[64,2176]{1,0:T(8,128)(2,1)S(1)}, bf16[64,2176]{1,0:T(8,128)(2,1)S(1)}, u32[]{:S(2)}, u32[]{:S(2)}) %collective-permute-start.2) | collective-permute-done | bytes 278560 | tf_op jit(solution)/shard_map/ppermute | solution.py:347
  54.3 0.0 collective-permute-done.1.refs_1_
  54.3 1.5 %shard_map.67 = (f32[16,72,128]{2,1,0:T(8,128)S(1)}, f32[8,256]{1,0:T(8,128)S(1)}) custom-call(bf16[16,16,2176]{2,1,0:T(8,128)(2,1)S(1)} %all_to_all.15.near_ref, bf16[16,16,2176]{2,1,0:T(8,128)(2,1)S(1)} %collective-permute-done.far_ref, bf16[512,512]{1,0:T(8,128)(2,1)S(1)} %get-tuple-element.14.move_ref, f32[512,128]{1,0:T(8,128)S(1)} %get-tuple-element.15.kind_ref, ...), custom_call_target="tpu_custom_call" | custom-call | tf_op jit(solution)/shard_map/pallas_call | solution.py:298
  55.8 28.3 %all_to_all.16 = f16[16,72,128]{2,1,0:T(8,128)(2,1)S(1)} all-to-all(f16[16,72,128]{2,1,0:T(8,128)(2,1)S(1)} %convert_element_type.6), channel_id=1, replica_groups=mesh['grp'=16,'row'=32] {'grp'}, dimensions={0} | all-to-all | bytes 589824 | tf_op jit(solution)/shard_map/all_to_all | solution.py:357
  84.3 0.7 shard_map.68
  84.9 18.4 %all_to_all.17 = f32[32,8,128]{2,1,0:T(8,128)S(1)} all-to-all(f32[32,8,128]{2,1,0:T(8,128)S(1)} %bitcast.8), channel_id=1, replica_groups=mesh['grp'=16,'row'=32] {'row'}, dimensions={0} | all-to-all | bytes 262144 | tf_op jit(solution)/shard_map/all_to_all | solution.py:360
  103.3 1.5 %shard_map.69 = f32[64,128]{1,0:T(8,128)} custom-call(f32[256,128]{1,0:T(8,128)S(1)} %bitcast.7), custom_call_target="tpu_custom_call" | custom-call | tf_op jit(solution)/shard_map/pallas_call | solution.py:298
  (4 shorter events, 0.1 us)
Async XLA Ops:
  24.5 18.1 %collective-permute-start = (bf16[16,16,2176]{2,1,0:T(8,128)(2,1)S(1)}, bf16[16,16,2176]{2,1,0:T(8,128)(2,1)S(1)}, u32[]{:S(2)}, u32[]{:S(2)}) collective-permute-start(bf16[16,16,2176]{2,1,0:T(8,128)(2,1)S(1)} %all_to_all.15.near_ref), channel_id=1, source_target_pairs={{0,1},{1,0},{2,3},{3,2},{4,5},{5,4},{6,7},{7,6},{8,9},{9,8},{10,11... | collective-permute-start | bytes 3342344 | tf_op jit(solution)/shard_map/ppermute | solution.py:348
  34.5 10.1 %collective-permute-start.3 = (bf16[64,2176]{1,0:T(8,128)(2,1)S(1)}, bf16[64,2176]{1,0:T(8,128)(2,1)S(1)}, u32[]{:S(2)}, u32[]{:S(2)}) collective-permute-start(bf16[64,2176]{1,0:T(8,128)(2,1)S(1)} %shard_map.66.refs_0_), channel_id=1, source_target_pairs={{0,24},{1,25},{2,26},{3,27},{4,28},{5,29},{6,30},{7,31},{8,0},{9,1... | collective-permute-start | bytes 835592 | tf_op jit(solution)/shard_map/ppermute | solution.py:347
  37.3 17.0 %collective-permute-start.2 = (bf16[64,2176]{1,0:T(8,128)(2,1)S(1)}, bf16[64,2176]{1,0:T(8,128)(2,1)S(1)}, u32[]{:S(2)}, u32[]{:S(2)}) collective-permute-start(bf16[64,2176]{1,0:T(8,128)(2,1)S(1)} %shard_map.66.refs_0_), channel_id=1, source_target_pairs={{0,8},{1,9},{2,10},{3,11},{4,12},{5,13},{6,14},{7,15},{8,16},{9,17... | collective-permute-start | bytes 835592 | tf_op jit(solution)/shard_map/ppermute | solution.py:347
  39.8 14.5 %collective-permute-start.1 = (bf16[64,2176]{1,0:T(8,128)(2,1)S(1)}, bf16[64,2176]{1,0:T(8,128)(2,1)S(1)}, u32[]{:S(2)}, u32[]{:S(2)}) collective-permute-start(bf16[64,2176]{1,0:T(8,128)(2,1)S(1)} %shard_map.66.refs_0_), channel_id=1, source_target_pairs={{0,16},{1,17},{2,18},{3,19},{4,20},{5,21},{6,22},{7,23},{8,24},{9,... | collective-permute-start | bytes 835592 | tf_op jit(solution)/shard_map/ppermute | solution.py:347

commit v7 on v6

--- a/solution.py
+++ b/solution.py
@@ -40,11 +40,9 @@
     return lax.dot_general(a, b, (((1,), (0,)), ((), ())), precision=precision, preferred_element_type=F32)
 
 
-def thirds(x):
+def halves_of(x):
     high = x.astype(BF16)
-    rest = x - high.astype(F32)
-    middle = rest.astype(BF16)
-    return high, middle, (rest - middle.astype(F32)).astype(BF16)
+    return high, (x - high.astype(F32)).astype(BF16)
 
 
 def folded(read, weigh):
@@ -238,10 +236,10 @@
     m = iota((256, 256), 0).astype(F32)
     hit = (m == target) | (m == target + 4.0)
     pick = jnp.concatenate([ones_where(hit & (rank == float(k)), BF16) for k in range(SIDE)], axis=0)
-    high, middle, low = thirds(total)
+    high, low = halves_of(total)
     inner = jnp.broadcast_to(row_ref[2:3, :], (16, 256)).astype(BF16)
     found = nt(pick, jnp.concatenate([high, inner], axis=0))
-    value = found[:, 0:32] + (nt(pick, middle) + nt(pick, low))
+    value = found[:, 0:32] + nt(pick, low)
     index = jnp.broadcast_to(found[:, 32:33], (4 * 256, 32))
     s = iota((512, 128), 0)
     lane = iota((512, 128), 1)
@@ -264,15 +262,15 @@
         [ones_where(is_value & (high[:, 32 * k : 32 * k + 1] == spot), BF16) for k in range(SIDE)], axis=1
     )
     found = None
-    for part in thirds(wide):
+    for part in halves_of(wide):
         term = tn(place, part)
         found = term if found is None else found + term
     total = jnp.where(lane == 0, found[0:64], jnp.where(lane == 1, found[64:128], jnp.where(lane == 2, found[128:192], found[192:256])))
     id_row = wide[4:5, :]
     col = id_row - 128.0 * jnp.floor(id_row * (1.0 / 128.0))
     spread = ones_where(iota((128, 512), 0).astype(F32) == col, BF16)
-    high, middle, low = thirds(total)
-    out_ref[...] = nt(high, spread) + (nt(middle, spread) + nt(low, spread))
+    high, low = halves_of(total)
+    out_ref[...] = nt(high, spread) + nt(low, spread)
 
 
 def near_by(*dims, dtype=F32):

time: 105 us -> 105 us (level)
  no operation moved by 1% of the time
where the time goes in v7:
time: 105 us; the launch traced here: 104 us
  blocking collectives  69.8 us (66%)
  starting transfers between devices  13.1 us (12%)
  waiting for transfers between devices  11 us (10%)
  Pallas kernels  10.4 us (10%)
    all_to_all x1, blocking collectives, shards(): arrived = lax.all_to_all(sent, 'grp', 0, 0, tiled=True).astype(F32)  28.3 us
    all_to_all x1, blocking collectives, shards(): lax.all_to_all(classes, 'row', 0, 0, tiled=True, axis_index_groups=PLANES)  23.1 us
    all_to_all x1, blocking collectives, shards(): lax.all_to_all(outgoing.reshape(32, 8, 128), 'row', 0, 0, tiled=True)  18.4 us
    ppermute x3, waiting for transfers between devices, shards(): lined.append(lax.ppermute(own, 'row', shift(n, 0)))  11 us
    pallas_call x6, Pallas kernels, placed(): run(*(pltpu.with_memory_space_constraint(a, pltpu.VMEM) if i in held else...  10.4 us
    ppermute x3, starting transfers between devices, shards(): lined.append(lax.ppermute(own, 'row', shift(n, 0)))  8.13 us
    ppermute x1, starting transfers between devices, shards(): far = lax.ppermute(near, 'row', SWAP)  5 us
  transfers between devices with their start and end apart: 4, of which 2 were waited for; matrix products, arithmetic and copies ran while one was open for 0% of the time, Pallas kernels for 5%

profile of v7, /device:TPU:1, one launch (start us, length us, event | category | flops | bytes accessed | tf_op | source)
XLA Modules:
  0.0 104.5 jit_solution(10053188045787039381)
XLA Ops:
  0.0 1.5 %shard_map.64 = bf16[16,16,2176]{2,1,0:T(8,128)(2,1)S(1)} custom-call(s32[1]{0:T(128)} %bitcast.me_ref, bf16[64,4096]{1,0:T(8,128)(2,1)} %bitcast.9, s32[1,64]{1,0:T(1,128)} %bitcast.12, s32[1,64]{1,0:T(1,128)} %touched_ref.3), custom_call_target="tpu_custom_call" | custom-call | tf_op jit(solution)/shard_map/pallas_call | solution.py:296
  1.5 23.1 %all_to_all.15.near_ref = bf16[16,16,2176]{2,1,0:T(8,128)(2,1)S(1)} all-to-all(bf16[16,16,2176]{2,1,0:T(8,128)(2,1)S(1)} %shard_map.64), channel_id=1, replica_groups={{0,2,4,6,8,10,12,14,16,18,20,22,24,26,28,30},{1,3,5,7,9,11,13,15,17,19,..., dimensions={0} | all-to-all | bytes 2228224 | tf_op jit(solution)/shard_map/all_to_all | solution.py:328
  24.5 5.0 %collective-permute-start = (bf16[16,16,2176]{2,1,0:T(8,128)(2,1)S(1)}, bf16[16,16,2176]{2,1,0:T(8,128)(2,1)S(1)}, u32[]{:S(2)}, u32[]{:S(2)}) collective-permute-start(bf16[16,16,2176]{2,1,0:T(8,128)(2,1)S(1)} %all_to_all.15.near_ref), channel_id=1, source_target_pairs={{0,1},{1,0},{2,3},{3,2},{4,5},{5,4},{6,7},{7,6},{8,9},{9,8},{10,11... | collective-permute-start | bytes 3342344 | tf_op jit(solution)/shard_map/ppermute | solution.py:346
  29.5 5.0 %shard_map.66.refs_0_ = bf16[64,2176]{1,0:T(8,128)(2,1)S(1)} custom-call(s32[1]{0:T(128)} %bitcast.me_ref, s32[1,64]{1,0:T(1,128)} %touched_ref.3, s32[8]{0:T(128)} %class_ref.1, bf16[64,4096]{1,0:T(8,128)(2,1)} %bitcast.10, bf16[8,64,64]{2,1,0:T(8,128)(2,1)} %x_ref.1, bf16[8,64,64]{2,1,0:T(8,128)(2,1)} %z_ref.1, s32[1,64]{1,0:T(1,128)} %bitcast.13, ...), custom_call_target="tpu_custom_call" | custom-call | tf_op jit(solution)/shard_map/pallas_call | solution.py:296
  34.5 2.8 %collective-permute-start.3 = (bf16[64,2176]{1,0:T(8,128)(2,1)S(1)}, bf16[64,2176]{1,0:T(8,128)(2,1)S(1)}, u32[]{:S(2)}, u32[]{:S(2)}) collective-permute-start(bf16[64,2176]{1,0:T(8,128)(2,1)S(1)} %shard_map.66.refs_0_), channel_id=1, source_target_pairs={{0,24},{1,25},{2,26},{3,27},{4,28},{5,29},{6,30},{7,31},{8,0},{9,1... | collective-permute-start | bytes 835592 | tf_op jit(solution)/shard_map/ppermute | solution.py:345
  37.3 2.5 %collective-permute-start.2 = (bf16[64,2176]{1,0:T(8,128)(2,1)S(1)}, bf16[64,2176]{1,0:T(8,128)(2,1)S(1)}, u32[]{:S(2)}, u32[]{:S(2)}) collective-permute-start(bf16[64,2176]{1,0:T(8,128)(2,1)S(1)} %shard_map.66.refs_0_), channel_id=1, source_target_pairs={{0,8},{1,9},{2,10},{3,11},{4,12},{5,13},{6,14},{7,15},{8,16},{9,17... | collective-permute-start | bytes 835592 | tf_op jit(solution)/shard_map/ppermute | solution.py:345
  39.8 2.8 %collective-permute-start.1 = (bf16[64,2176]{1,0:T(8,128)(2,1)S(1)}, bf16[64,2176]{1,0:T(8,128)(2,1)S(1)}, u32[]{:S(2)}, u32[]{:S(2)}) collective-permute-start(bf16[64,2176]{1,0:T(8,128)(2,1)S(1)} %shard_map.66.refs_0_), channel_id=1, source_target_pairs={{0,16},{1,17},{2,18},{3,19},{4,20},{5,21},{6,22},{7,23},{8,24},{9,... | collective-permute-start | bytes 835592 | tf_op jit(solution)/shard_map/ppermute | solution.py:345
  42.7 0.0 collective-permute-done.far_ref
  42.7 0.6 shard_map.65
  43.3 1.3 %collective-permute-done.3.refs_3_ = bf16[64,2176]{1,0:T(8,128)(2,1)S(1)} collective-permute-done((bf16[64,2176]{1,0:T(8,128)(2,1)S(1)}, bf16[64,2176]{1,0:T(8,128)(2,1)S(1)}, u32[]{:S(2)}, u32[]{:S(2)}) %collective-permute-start.3) | collective-permute-done | bytes 278560 | tf_op jit(solution)/shard_map/ppermute | solution.py:345
  44.6 9.7 %collective-permute-done.2.refs_2_ = bf16[64,2176]{1,0:T(8,128)(2,1)S(1)} collective-permute-done((bf16[64,2176]{1,0:T(8,128)(2,1)S(1)}, bf16[64,2176]{1,0:T(8,128)(2,1)S(1)}, u32[]{:S(2)}, u32[]{:S(2)}) %collective-permute-start.2) | collective-permute-done | bytes 278560 | tf_op jit(solution)/shard_map/ppermute | solution.py:345
  54.3 0.0 collective-permute-done.1.refs_1_
  54.3 1.5 %shard_map.67 = (f32[16,72,128]{2,1,0:T(8,128)S(1)}, f32[8,256]{1,0:T(8,128)S(1)}) custom-call(bf16[16,16,2176]{2,1,0:T(8,128)(2,1)S(1)} %all_to_all.15.near_ref, bf16[16,16,2176]{2,1,0:T(8,128)(2,1)S(1)} %collective-permute-done.far_ref, bf16[512,512]{1,0:T(8,128)(2,1)S(1)} %get-tuple-element.14.move_ref, f32[512,128]{1,0:T(8,128)S(1)} %get-tuple-element.15.kind_ref, ...), custom_call_target="tpu_custom_call" | custom-call | tf_op jit(solution)/shard_map/pallas_call | solution.py:296
  55.8 28.3 %all_to_all.16 = f16[16,72,128]{2,1,0:T(8,128)(2,1)S(1)} all-to-all(f16[16,72,128]{2,1,0:T(8,128)(2,1)S(1)} %convert_element_type.6), channel_id=1, replica_groups=mesh['grp'=16,'row'=32] {'grp'}, dimensions={0} | all-to-all | bytes 589824 | tf_op jit(solution)/shard_map/all_to_all | solution.py:355
  84.3 0.5 shard_map.68
  84.8 18.4 %all_to_all.17 = f32[32,8,128]{2,1,0:T(8,128)S(1)} all-to-all(f32[32,8,128]{2,1,0:T(8,128)S(1)} %bitcast.8), channel_id=1, replica_groups=mesh['grp'=16,'row'=32] {'row'}, dimensions={0} | all-to-all | bytes 262144 | tf_op jit(solution)/shard_map/all_to_all | solution.py:358
  103.1 1.3 %shard_map.69 = f32[64,128]{1,0:T(8,128)} custom-call(f32[256,128]{1,0:T(8,128)S(1)} %bitcast.7), custom_call_target="tpu_custom_call" | custom-call | tf_op jit(solution)/shard_map/pallas_call | solution.py:296
  (4 shorter events, 0.1 us)
Async XLA Ops:
  24.5 18.1 %collective-permute-start = (bf16[16,16,2176]{2,1,0:T(8,128)(2,1)S(1)}, bf16[16,16,2176]{2,1,0:T(8,128)(2,1)S(1)}, u32[]{:S(2)}, u32[]{:S(2)}) collective-permute-start(bf16[16,16,2176]{2,1,0:T(8,128)(2,1)S(1)} %all_to_all.15.near_ref), channel_id=1, source_target_pairs={{0,1},{1,0},{2,3},{3,2},{4,5},{5,4},{6,7},{7,6},{8,9},{9,8},{10,11... | collective-permute-start | bytes 3342344 | tf_op jit(solution)/shard_map/ppermute | solution.py:346
  34.5 10.1 %collective-permute-start.3 = (bf16[64,2176]{1,0:T(8,128)(2,1)S(1)}, bf16[64,2176]{1,0:T(8,128)(2,1)S(1)}, u32[]{:S(2)}, u32[]{:S(2)}) collective-permute-start(bf16[64,2176]{1,0:T(8,128)(2,1)S(1)} %shard_map.66.refs_0_), channel_id=1, source_target_pairs={{0,24},{1,25},{2,26},{3,27},{4,28},{5,29},{6,30},{7,31},{8,0},{9,1... | collective-permute-start | bytes 835592 | tf_op jit(solution)/shard_map/ppermute | solution.py:345
  37.3 17.0 %collective-permute-start.2 = (bf16[64,2176]{1,0:T(8,128)(2,1)S(1)}, bf16[64,2176]{1,0:T(8,128)(2,1)S(1)}, u32[]{:S(2)}, u32[]{:S(2)}) collective-permute-start(bf16[64,2176]{1,0:T(8,128)(2,1)S(1)} %shard_map.66.refs_0_), channel_id=1, source_target_pairs={{0,8},{1,9},{2,10},{3,11},{4,12},{5,13},{6,14},{7,15},{8,16},{9,17... | collective-permute-start | bytes 835592 | tf_op jit(solution)/shard_map/ppermute | solution.py:345
  39.8 14.5 %collective-permute-start.1 = (bf16[64,2176]{1,0:T(8,128)(2,1)S(1)}, bf16[64,2176]{1,0:T(8,128)(2,1)S(1)}, u32[]{:S(2)}, u32[]{:S(2)}) collective-permute-start(bf16[64,2176]{1,0:T(8,128)(2,1)S(1)} %shard_map.66.refs_0_), channel_id=1, source_target_pairs={{0,16},{1,17},{2,18},{3,19},{4,20},{5,21},{6,22},{7,23},{8,24},{9,... | collective-permute-start | bytes 835592 | tf_op jit(solution)/shard_map/ppermute | solution.py:345

commit v8 on v7

--- a/solution.py
+++ b/solution.py
@@ -179,7 +179,7 @@
         out_ref[:, q * 128 : (q + 1) * 128] = chunk.astype(BF16)
 
 
-def order_kernel(near_ref, far_ref, move_ref, kind_ref, col_ref):
+def order_kernel(near_ref, far_ref, sorted_ref, kind_ref, col_ref):
     n_cols = 512
     last = slice(16 * 128, WIDTH)
     ids = [ref[:, :, last].reshape(256, 128) for ref in (near_ref, far_ref)]
@@ -190,20 +190,19 @@
     rank = jnp.sum(jnp.where(col_f[:, 3:4] < col_t[3:4, :], nt(own, own), 0.0), axis=0, keepdims=True)
     place = col_t[1:2, :] * 16.0 + rank
     move = ones_where(iota((n_cols, n_cols), 0).astype(F32) == place, BF16)
-    move_ref[...] = move
-    kind_ref[...] = col_f
+    every = jnp.concatenate([near_ref[...].reshape(256, WIDTH), far_ref[...].reshape(256, WIDTH)], axis=0)
+    sorted_ref[...] = nn(move, every).astype(BF16)
+    kind_ref[...] = nn(move, col_ids)
     odd = col_t[1:2, :] - 2.0 * jnp.floor(col_t[1:2, :] * 0.5)
     col_id = (odd * 64.0 + col_t[2:3, :]).astype(BF16)
     col_ref[...] = nt(jnp.broadcast_to(col_id, (8, n_cols)), move)
 
 
-def score_kernel(near_ref, far_ref, move_ref, kind_ref, *refs):
+def score_kernel(sorted_ref, kind_ref, *refs):
     row_refs, (out_ref, row_ref) = refs[:SIDE], refs[SIDE:]
     n_rows = 256
     rows = jnp.concatenate([ref[...] for ref in row_refs], axis=0)
-    near = near_ref[...].reshape(256, WIDTH)
-    far = far_ref[...].reshape(256, WIDTH)
-    scores = jnp.concatenate([nt(near, rows), nt(far, rows)], axis=0)
+    scores = nt(sorted_ref[...], rows)
     row_ids = rows[:, 16 * 128 :]
     row_t = nt(ones_where(iota((8, 128), 0) + 4 == iota((8, 128), 1), BF16), row_ids)
     row_f = row_ids.astype(F32)
@@ -214,14 +213,10 @@
     row_ref[1:2, :] = row_rank
     row_ref[2:3, :] = row_t[2:3, :] + 1.0
     row_ref[3:8, :] = jnp.zeros((5, n_rows), F32)
-    move = move_ref[...]
     scores = jnp.where(kind_ref[:, 0:1] == row_t[0:1, :], scores, 0.0)
     top = jnp.max(jnp.max(jnp.abs(scores), axis=0, keepdims=True), axis=1, keepdims=True)
     power = jnp.minimum(jnp.ceil(jnp.log(jnp.maximum(top, 1e-36)) * 1.4426950408889634), 126.0)
-    scaled = scores * jnp.exp2(-power)
-    high = scaled.astype(BF16)
-    low = (scaled - high.astype(F32)).astype(BF16)
-    moved = nn(move, high) + nn(move, low)
+    moved = scores * jnp.exp2(-power)
     note = jnp.broadcast_to(power + 1.0, (8, 128))
     for g in range(16):
         out_ref[g, 0:32, :] = moved[32 * g : 32 * (g + 1), 0:128]
@@ -344,11 +339,11 @@
     for n in (2, 1, 3):
         lined.append(lax.ppermute(own, "row", shift(n, 0)))
     far = lax.ppermute(near, "row", SWAP)
-    move, kinds, cols = call(
-        order_kernel, (near_by(512, 512, dtype=BF16), near_by(512, 128), near_by(8, 512)), 2, held=(0, 1)
+    columns, kinds, cols = call(
+        order_kernel, (near_by(512, WIDTH, dtype=BF16), near_by(512, 128), near_by(8, 512)), 2, held=(0, 1)
     )(near, far)
-    scores, rows = call(score_kernel, (near_by(16, SLAB, 128), near_by(8, 256)), 4 + SIDE, held=tuple(range(4 + SIDE)))(
-        near, far, move, kinds, *lined
+    scores, rows = call(score_kernel, (near_by(16, SLAB, 128), near_by(8, 256)), 2 + SIDE, held=tuple(range(2 + SIDE)))(
+        columns, kinds, *lined
     )
     group = lax.axis_index("grp").astype(jnp.int32).reshape(1)
     sent, cols, rows, group = lax.optimization_barrier((scores.astype(jnp.float16), cols, rows, group))

time: 105 us -> 102 us (0.971)
  waiting for transfers between devices: 11 us -> 6.72 us
  starting transfers between devices: 13.1 us -> 14.3 us
    ppermute x3, waiting for transfers between devices: 11 us -> 6.72 us  [shards(): lined.append(lax.ppermute(own, 'row', shift(n, 0)))]
    ppermute x3, starting transfers between devices: 8.13 us -> 9.34 us  [shards(): lined.append(lax.ppermute(own, 'row', shift(n, 0)))]
    all_to_all x1, blocking collectives: 18.4 us -> 17.2 us  [shards(): lax.all_to_all(outgoing.reshape(32, 8, 128), 'row', 0, 0, tiled=True)]
  transfers between devices with their start and end apart: 4 -> 4, of which waited for: 2 -> 2; matrix products, arithmetic and copies ran while one was open for 0% -> 0% of each run, Pallas kernels for 5% -> 7%
where the time goes in v8:
time: 102 us
  blocking collectives  69.4 us (68%)
  starting transfers between devices  14.3 us (14%)
  Pallas kernels  11.1 us (11%)
  waiting for transfers between devices  6.72 us (7%)
    all_to_all x1, blocking collectives, shards(): arrived = lax.all_to_all(sent, 'grp', 0, 0, tiled=True).astype(F32)  29.2 us
    all_to_all x1, blocking collectives, shards(): lax.all_to_all(classes, 'row', 0, 0, tiled=True, axis_index_groups=PLANES)  23.1 us
    all_to_all x1, blocking collectives, shards(): lax.all_to_all(outgoing.reshape(32, 8, 128), 'row', 0, 0, tiled=True)  17.2 us
    pallas_call x6, Pallas kernels, placed(): run(*(pltpu.with_memory_space_constraint(a, pltpu.VMEM) if i in held else...  11.1 us
    ppermute x3, starting transfers between devices, shards(): lined.append(lax.ppermute(own, 'row', shift(n, 0)))  9.34 us
    ppermute x3, waiting for transfers between devices, shards(): lined.append(lax.ppermute(own, 'row', shift(n, 0)))  6.72 us
    ppermute x1, starting transfers between devices, shards(): far = lax.ppermute(near, 'row', SWAP)  5 us
  transfers between devices with their start and end apart: 4, of which 2 were waited for; matrix products, arithmetic and copies ran while one was open for 0% of the time, Pallas kernels for 7%

profile of v8, /device:TPU:1, one launch (start us, length us, event | category | flops | bytes accessed | tf_op | source)
XLA Modules:
  0.0 101.9 jit_solution(17022886175756652186)
XLA Ops:
  0.0 1.5 %shard_map.64 = bf16[16,16,2176]{2,1,0:T(8,128)(2,1)S(1)} custom-call(s32[1]{0:T(128)} %bitcast.me_ref, bf16[64,4096]{1,0:T(8,128)(2,1)} %bitcast.9, s32[1,64]{1,0:T(1,128)} %bitcast.12, s32[1,64]{1,0:T(1,128)} %touched_ref.3), custom_call_target="tpu_custom_call" | custom-call | tf_op jit(solution)/shard_map/pallas_call | solution.py:291
  1.5 23.1 %all_to_all.15.near_ref = bf16[16,16,2176]{2,1,0:T(8,128)(2,1)S(1)} all-to-all(bf16[16,16,2176]{2,1,0:T(8,128)(2,1)S(1)} %shard_map.64), channel_id=1, replica_groups={{0,2,4,6,8,10,12,14,16,18,20,22,24,26,28,30},{1,3,5,7,9,11,13,15,17,19,..., dimensions={0} | all-to-all | bytes 2228224 | tf_op jit(solution)/shard_map/all_to_all | solution.py:323
  24.5 5.0 %collective-permute-start = (bf16[16,16,2176]{2,1,0:T(8,128)(2,1)S(1)}, bf16[16,16,2176]{2,1,0:T(8,128)(2,1)S(1)}, u32[]{:S(2)}, u32[]{:S(2)}) collective-permute-start(bf16[16,16,2176]{2,1,0:T(8,128)(2,1)S(1)} %all_to_all.15.near_ref), channel_id=1, source_target_pairs={{0,1},{1,0},{2,3},{3,2},{4,5},{5,4},{6,7},{7,6},{8,9},{9,8},{10,11... | collective-permute-start | bytes 3342344 | tf_op jit(solution)/shard_map/ppermute | solution.py:341
  29.5 5.0 %shard_map.66.refs_0_ = bf16[64,2176]{1,0:T(8,128)(2,1)S(1)} custom-call(s32[1]{0:T(128)} %bitcast.me_ref, s32[1,64]{1,0:T(1,128)} %touched_ref.3, s32[8]{0:T(128)} %class_ref.1, bf16[64,4096]{1,0:T(8,128)(2,1)} %bitcast.10, bf16[8,64,64]{2,1,0:T(8,128)(2,1)} %x_ref.1, bf16[8,64,64]{2,1,0:T(8,128)(2,1)} %z_ref.1, s32[1,64]{1,0:T(1,128)} %bitcast.13, ...), custom_call_target="tpu_custom_call" | custom-call | tf_op jit(solution)/shard_map/pallas_call | solution.py:291
  34.5 2.8 %collective-permute-start.1 = (bf16[64,2176]{1,0:T(8,128)(2,1)S(1)}, bf16[64,2176]{1,0:T(8,128)(2,1)S(1)}, u32[]{:S(2)}, u32[]{:S(2)}) collective-permute-start(bf16[64,2176]{1,0:T(8,128)(2,1)S(1)} %shard_map.66.refs_0_), channel_id=1, source_target_pairs={{0,16},{1,17},{2,18},{3,19},{4,20},{5,21},{6,22},{7,23},{8,24},{9,... | collective-permute-start | bytes 835592 | tf_op jit(solution)/shard_map/ppermute | solution.py:340
  37.4 2.4 %collective-permute-start.2 = (bf16[64,2176]{1,0:T(8,128)(2,1)S(1)}, bf16[64,2176]{1,0:T(8,128)(2,1)S(1)}, u32[]{:S(2)}, u32[]{:S(2)}) collective-permute-start(bf16[64,2176]{1,0:T(8,128)(2,1)S(1)} %shard_map.66.refs_0_), channel_id=1, source_target_pairs={{0,8},{1,9},{2,10},{3,11},{4,12},{5,13},{6,14},{7,15},{8,16},{9,17... | collective-permute-start | bytes 835592 | tf_op jit(solution)/shard_map/ppermute | solution.py:340
  39.8 4.1 %collective-permute-start.3 = (bf16[64,2176]{1,0:T(8,128)(2,1)S(1)}, bf16[64,2176]{1,0:T(8,128)(2,1)S(1)}, u32[]{:S(2)}, u32[]{:S(2)}) collective-permute-start(bf16[64,2176]{1,0:T(8,128)(2,1)S(1)} %shard_map.66.refs_0_), channel_id=1, source_target_pairs={{0,24},{1,25},{2,26},{3,27},{4,28},{5,29},{6,30},{7,31},{8,0},{9,1... | collective-permute-start | bytes 835592 | tf_op jit(solution)/shard_map/ppermute | solution.py:340
  43.9 0.0 collective-permute-done.far_ref
  43.9 1.9 %shard_map.65 = (bf16[512,2176]{1,0:T(8,128)(2,1)S(1)}, f32[512,128]{1,0:T(8,128)S(1)}, f32[8,512]{1,0:T(8,128)S(1)}) custom-call(bf16[16,16,2176]{2,1,0:T(8,128)(2,1)S(1)} %all_to_all.15.near_ref, bf16[16,16,2176]{2,1,0:T(8,128)(2,1)S(1)} %collective-permute-done.far_ref), custom_call_target="tpu_custom_call" | custom-call | tf_op jit(solution)/shard_map/pallas_call | solution.py:291
  45.8 0.4 collective-permute-done.1.refs_1_
  46.2 6.3 %collective-permute-done.2.refs_2_ = bf16[64,2176]{1,0:T(8,128)(2,1)S(1)} collective-permute-done((bf16[64,2176]{1,0:T(8,128)(2,1)S(1)}, bf16[64,2176]{1,0:T(8,128)(2,1)S(1)}, u32[]{:S(2)}, u32[]{:S(2)}) %collective-permute-start.2) | collective-permute-done | bytes 278560 | tf_op jit(solution)/shard_map/ppermute | solution.py:340
  52.5 0.0 collective-permute-done.3.refs_3_
  52.5 1.0 shard_map.67
  53.6 29.2 %all_to_all.16 = f16[16,72,128]{2,1,0:T(8,128)(2,1)S(1)} all-to-all(f16[16,72,128]{2,1,0:T(8,128)(2,1)S(1)} %convert_element_type.6), channel_id=1, replica_groups=mesh['grp'=16,'row'=32] {'grp'}, dimensions={0} | all-to-all | bytes 589824 | tf_op jit(solution)/shard_map/all_to_all | solution.py:350
  82.8 0.5 shard_map.68
  83.3 17.2 %all_to_all.17 = f32[32,8,128]{2,1,0:T(8,128)S(1)} all-to-all(f32[32,8,128]{2,1,0:T(8,128)S(1)} %bitcast.8), channel_id=1, replica_groups=mesh['grp'=16,'row'=32] {'row'}, dimensions={0} | all-to-all | bytes 262144 | tf_op jit(solution)/shard_map/all_to_all | solution.py:353
  100.5 1.3 %shard_map.69 = f32[64,128]{1,0:T(8,128)} custom-call(f32[256,128]{1,0:T(8,128)S(1)} %bitcast.7), custom_call_target="tpu_custom_call" | custom-call | tf_op jit(solution)/shard_map/pallas_call | solution.py:291
  (4 shorter events, 0.1 us)
Async XLA Ops:
  24.5 19.3 %collective-permute-start = (bf16[16,16,2176]{2,1,0:T(8,128)(2,1)S(1)}, bf16[16,16,2176]{2,1,0:T(8,128)(2,1)S(1)}, u32[]{:S(2)}, u32[]{:S(2)}) collective-permute-start(bf16[16,16,2176]{2,1,0:T(8,128)(2,1)S(1)} %all_to_all.15.near_ref), channel_id=1, source_target_pairs={{0,1},{1,0},{2,3},{3,2},{4,5},{5,4},{6,7},{7,6},{8,9},{9,8},{10,11... | collective-permute-start | bytes 3342344 | tf_op jit(solution)/shard_map/ppermute | solution.py:341
  34.5 11.6 %collective-permute-start.1 = (bf16[64,2176]{1,0:T(8,128)(2,1)S(1)}, bf16[64,2176]{1,0:T(8,128)(2,1)S(1)}, u32[]{:S(2)}, u32[]{:S(2)}) collective-permute-start(bf16[64,2176]{1,0:T(8,128)(2,1)S(1)} %shard_map.66.refs_0_), channel_id=1, source_target_pairs={{0,16},{1,17},{2,18},{3,19},{4,20},{5,21},{6,22},{7,23},{8,24},{9,... | collective-permute-start | bytes 835592 | tf_op jit(solution)/shard_map/ppermute | solution.py:340
  37.4 15.1 %collective-permute-start.2 = (bf16[64,2176]{1,0:T(8,128)(2,1)S(1)}, bf16[64,2176]{1,0:T(8,128)(2,1)S(1)}, u32[]{:S(2)}, u32[]{:S(2)}) collective-permute-start(bf16[64,2176]{1,0:T(8,128)(2,1)S(1)} %shard_map.66.refs_0_), channel_id=1, source_target_pairs={{0,8},{1,9},{2,10},{3,11},{4,12},{5,13},{6,14},{7,15},{8,16},{9,17... | collective-permute-start | bytes 835592 | tf_op jit(solution)/shard_map/ppermute | solution.py:340
  39.8 12.7 %collective-permute-start.3 = (bf16[64,2176]{1,0:T(8,128)(2,1)S(1)}, bf16[64,2176]{1,0:T(8,128)(2,1)S(1)}, u32[]{:S(2)}, u32[]{:S(2)}) collective-permute-start(bf16[64,2176]{1,0:T(8,128)(2,1)S(1)} %shard_map.66.refs_0_), channel_id=1, source_target_pairs={{0,24},{1,25},{2,26},{3,27},{4,28},{5,29},{6,30},{7,31},{8,0},{9,1... | collective-permute-start | bytes 835592 | tf_op jit(solution)/shard_map/ppermute | solution.py:340
